TPU v7x, 256 devices: a whole 4x4x8 slice. The times are simulated.
256 devices in a mesh: gx: 4 (over x), gy: 4 (over y_lo, core), gz: 16 (over z, y_hi).
Axes of the slice: x: 4, y: 4 (y_hi: 2, y_lo: 2; y = y_hi * 2 + y_lo), z: 8, core: 2. Of those that a mesh axis runs over, the one named last changes fastest.
Arguments:
- left_modes: bfloat16 [2, 4, 2, 128, 3, 131072], P(None, None, None, None, None, ('gx', 'gy', 'gz')), may hold values from -0.14160156 to 0.14160156
- right_modes: bfloat16 [2, 4, 2, 128, 3, 131072], P(None, None, None, None, None, ('gx', 'gy', 'gz')), may hold values from -0.14160156 to 0.14160156
- gamma_cols: int32 [16, 4], replicated, may hold values from 0 to 3, each once within a row
- gamma_phase: int32 [16, 4], replicated, may hold values from 0 to 3
- dilution: int32 [64], replicated, may hold values from 0 to 3
- time_pairs: int32 [4, 2], replicated, may hold values from 0 to 1
Outputs:
- meson_fields: float32 [16, 2, 2, 128, 128], P('gz', None, None, ('gx', 'gy'))
- traces: float32 [4, 16, 16, 2], P(None, 'gz')
Inputs may be any that keep to these rules, and one draw needn't show every extreme that they name: Each row of gamma_cols is a permutation of the four spins.
All inputs are finite; a program needn't handle non-finite values.
Results may differ from a plain program's by a relative error of at most 0.0003.
Values sent between devices are 32-bit elements; how exact they have to be, the bound alone decides.
No kernel may reach another device: no remote copies, remote signals or barrier semaphores. Data moves between devices by JAX's collectives and lax.ppermute only.
A program may use at most 128 MiB of HBM per device.

v0:
```python
import jax
import jax.numpy as jnp
from jax import lax
from jax.sharding import PartitionSpec as P

EXACT = lax.Precision.HIGHEST


def coefficients(gamma_cols, gamma_phase):
    spin_ids = jnp.arange(4, dtype=jnp.int32)
    onehot = (gamma_cols[:, :, None] == spin_ids[None, None, :]).astype(jnp.float32)
    real_sign = (gamma_phase == 0).astype(jnp.float32) - (gamma_phase == 2).astype(jnp.float32)
    imag_sign = (gamma_phase == 1).astype(jnp.float32) - (gamma_phase == 3).astype(jnp.float32)
    return (onehot * real_sign[:, :, None], onehot * imag_sign[:, :, None])


def select_pairs(crossed, time_pairs):
    time_ids = jnp.arange(crossed.shape[1], dtype=jnp.int32)
    first_time = (time_pairs[:, 0:1] == time_ids[None, :]).astype(jnp.float32)
    second_time = (time_pairs[:, 1:2] == time_ids[None, :]).astype(jnp.float32)
    chosen = jnp.einsum("pt,pu,gtahub->pgahb", first_time, second_time, crossed, precision=EXACT)
    real_part = chosen[:, :, 0, :, 0] - chosen[:, :, 1, :, 1]
    imag_part = chosen[:, :, 0, :, 1] + chosen[:, :, 1, :, 0]
    return jnp.stack([real_part, imag_part], axis=-1)


def project(coef_re, coef_im, pair_re, pair_im, form, part_axis):
    meson_re = jnp.einsum(form, coef_re, pair_re, precision=EXACT) - jnp.einsum(
        form, coef_im, pair_im, precision=EXACT
    )
    meson_im = jnp.einsum(form, coef_re, pair_im, precision=EXACT) + jnp.einsum(
        form, coef_im, pair_re, precision=EXACT
    )
    return jnp.stack([meson_re, meson_im], axis=part_axis)


def finish_whole(summed, time_pairs, local_gammas, block_rows, mode_count):
    group_start = lax.axis_index("gz") * local_gammas
    my_gammas = lax.dynamic_slice_in_dim(summed, group_start, local_gammas, 0)
    row_block = lax.axis_index("gx") * lax.axis_size("gy") + lax.axis_index("gy")
    meson_fields = lax.dynamic_slice_in_dim(my_gammas, row_block * block_rows, block_rows, 3)
    crossed = jnp.einsum("gtaij,hubji->gtahub", my_gammas, summed, precision=EXACT)
    traces = select_pairs(crossed, time_pairs) / mode_count
    return (meson_fields, traces)


def local(left_modes, right_modes, gamma_cols, gamma_phase, dilution, time_pairs):
    times_held = left_modes.shape[0]
    mode_count = left_modes.shape[3]
    gamma_count = gamma_cols.shape[0]
    noise_count = dilution.shape[0]
    low_count = mode_count - noise_count
    coef_re, coef_im = coefficients(gamma_cols, gamma_phase)
    groups = lax.axis_size("gz")
    blocks = lax.axis_size("gx") * lax.axis_size("gy")
    local_gammas = gamma_count // groups
    block_rows = mode_count // blocks
    spin_ids = jnp.arange(4, dtype=jnp.int32)
    noise_onehot = dilution[None, :] == spin_ids[:, None]
    select_table = noise_onehot.astype(jnp.bfloat16)
    low_re_list = []
    low_im_list = []
    noise_re_list = []
    noise_im_list = []
    for time_slot in range(times_held):
        left_slot = left_modes[time_slot]
        right_slot = right_modes[time_slot]
        low_prod = jnp.einsum(
            "spicx,qrjcx->sqpirj",
            left_slot,
            right_slot[:, :, :low_count],
            preferred_element_type=jnp.float32,
        )
        noise_right = jnp.sum(
            right_slot[:, :, low_count:] * select_table[:, None, :, None, None], axis=0
        )
        noise_prod = jnp.einsum(
            "spicx,qjcx->spiqj", left_slot, noise_right, preferred_element_type=jnp.float32
        )
        low_re_list.append(low_prod[:, :, 0, :, 0, :] + low_prod[:, :, 1, :, 1, :])
        low_im_list.append(low_prod[:, :, 0, :, 1, :] - low_prod[:, :, 1, :, 0, :])
        noise_re_list.append(noise_prod[:, 0, :, 0, :] + noise_prod[:, 1, :, 1, :])
        noise_im_list.append(noise_prod[:, 0, :, 1, :] - noise_prod[:, 1, :, 0, :])
    low_re, low_im, noise_re, noise_im = lax.psum(
        (
            jnp.stack(low_re_list),
            jnp.stack(low_im_list),
            jnp.stack(noise_re_list),
            jnp.stack(noise_im_list),
        ),
        ("gx", "gy", "gz"),
    )
    noise_float = noise_onehot.astype(jnp.float32)
    noise_coef_re = jnp.einsum("gsr,rj->gsj", coef_re, noise_float, precision=EXACT)
    noise_coef_im = jnp.einsum("gsr,rj->gsj", coef_im, noise_float, precision=EXACT)
    low_part = project(coef_re, coef_im, low_re, low_im, "gsr,tsrij->gtij", 2)
    noise_part = project(noise_coef_re, noise_coef_im, noise_re, noise_im, "gsj,tsij->gtij", 2)
    summed = jnp.concatenate([low_part, noise_part], axis=4)
    meson_fields, traces = finish_whole(summed, time_pairs, local_gammas, block_rows, mode_count)
    return (meson_fields, traces)


def solution(mesh):
    return jax.shard_map(
        local,
        mesh=mesh,
        in_specs=(
            P(None, None, None, None, None, ("gx", "gy", "gz")),
            P(None, None, None, None, None, ("gx", "gy", "gz")),
            P(),
            P(),
            P(),
            P(),
        ),
        out_specs=(P("gz", None, None, ("gx", "gy"), None), P(None, "gz", None, None)),
        check_vma=False,
    )
```

profile of v0, /device:TPU:1, one launch (start us, length us, event | category | flops | bytes accessed | tf_op | source)
XLA Modules:
  0.0 339.6 jit_solution(10529417758410979270)
XLA Ops:
  7.2 3.5 %slice_bitcast_fusion = (bf16[4,2,128,3,512]{4,2,3,1,0:T(8,128)(2,1)S(1)}, bf16[4,2,128,3,512]{4,2,3,1,0:T(8,128)(2,1)S(1)}) fusion(bf16[2,4,2,128,3,512]{5,3,4,2,1,0:T(8,128)(2,1)} %param.7), kind=kLoop, calls=%fused_computation.11 | loop fusion | bytes 12582912 | tf_op jit(solution)/shard_map/squeeze | solution.py:67
  10.7 1.1 copy-done.3
  11.9 0.7 slice_bitcast_fusion.3
  12.6 0.9 fusion.19
  13.5 1.1 fusion.30
  14.7 1.8 fusion.15
  16.7 1.1 fusion.27
  17.8 1.8 fusion.12
  19.8 0.8 pad_maximum_fusion.2
  20.6 1.5 pad_maximum_fusion
  22.9 267.7 %all-reduce.3.cloned.1.call-done = (f32[2,4,128,64]{2,3,1,0:T(8,128)}, f32[2,4,128,64]{2,3,1,0:T(8,128)}, f32[2,4,4,128,64]{3,4,1,2,0:T(8,128)}, f32[2,4,4,128,64]{3,4,1,2,0:T(8,128)}) async-done(((f32[2,4,128,64]{2,3,1,0:T(8,128)}, f32[2,4,128,64]{2,3,1,0:T(8,128)}, f32[2,4,4,128,64]{3,4,1,2,0:T(8,128)}, f32[2,4,4,128,64]{3,4,1,2,0:T(8,128)}), (f32[2,4,128,64]{2,3,1,0:T(8,128)}, ...) | async-done | bytes 2621456 | tf_op jit(solution)/shard_map/psum | solution.py:84
  290.7 3.3 convolution_bitcast_fusion.2
  294.0 3.3 convolution_bitcast_fusion
  297.3 2.0 fusion.24
  299.3 2.2 fusion.26
  301.5 1.2 fusion.48
  302.7 1.2 fusion.44
  303.9 1.2 fusion.22
  305.1 1.2 fusion.21
  306.2 2.7 fusion.101
  308.9 2.0 copy-done
  311.2 17.7 %fusion = f32[2,2,16,2,2,1]{2,1,5,4,3,0:T(2,128)S(1)} fusion(f32[2,2,128,128,1,1]{3,1,2,5,4,0:T(2,128)S(1)} %copy.67, f32[16,2,2,128,128,1]{3,0,4,1,2,5:T(8,128)} %get-tuple-element.14), kind=kOutput, calls=%fused_computation.1 | convolution fusion | flops 50331648 | bytes 4457472 | tf_op jit(solution)/shard_map/gtaij,hubji->gtahub/dot_general | solution.py:42
  329.8 2.2 constant_dynamic-slice_fusion.1
  332.0 0.7 copy.34
  (40 shorter events, 2.2 us)
Async XLA Ops:
  7.2 3.6 %copy-start.7 = (s32[64]{0:T(128)S(1)}, s32[64]{0:T(128)}, u32[]{:S(2)}) copy-start(s32[64]{0:T(128)} %param.10) | copy-start | bytes 772
  7.2 283.5 %all-reduce.3.cloned.1.call-start = ((), (), s32[]{:S(2)}) async-start(), calls=%async_computation | async-start | bytes 5242880 | tf_op jit(solution)/shard_map/psum | solution.py:84
  7.2 4.6 %copy-start.3 = (bf16[2,4,2,128,3,512]{5,3,4,2,1,0:T(8,128)(2,1)S(1)}, bf16[2,4,2,128,3,512]{5,3,4,2,1,0:T(8,128)(2,1)}, u32[]{:S(2)}) copy-start(bf16[2,4,2,128,3,512]{5,3,4,2,1,0:T(8,128)(2,1)} %param.6) | copy-start | bytes 18874372
  20.6 1.5 copy-start.8
  20.6 1.6 copy-start.6
  20.6 2.3 copy-start.9
  290.7 6.6 %copy-start.2 = (f32[2,4,4,128,64]{3,4,1,2,0:T(8,128)S(1)}, f32[2,4,4,128,64]{3,4,1,2,0:T(8,128)}, u32[]{:S(2)}) copy-start(f32[2,4,4,128,64]{3,4,1,2,0:T(8,128)} %get-tuple-element.8) | copy-start | bytes 3145732
  294.0 5.4 %copy-start.1 = (f32[2,4,4,128,64]{3,4,1,2,0:T(8,128)S(1)}, f32[2,4,4,128,64]{3,4,1,2,0:T(8,128)}, u32[]{:S(2)}) copy-start(f32[2,4,4,128,64]{3,4,1,2,0:T(8,128)} %get-tuple-element.9) | copy-start | bytes 3145732
  297.3 4.2 %copy-start.4 = (f32[2,4,128,64]{2,3,1,0:T(8,128)S(1)}, f32[2,4,128,64]{2,3,1,0:T(8,128)}, u32[]{:S(2)}) copy-start(f32[2,4,128,64]{2,3,1,0:T(8,128)} %get-tuple-element.7) | copy-start | bytes 786436
  297.3 5.4 %copy-start.5 = (f32[2,4,128,64]{2,3,1,0:T(8,128)S(1)}, f32[2,4,128,64]{2,3,1,0:T(8,128)}, u32[]{:S(2)}) copy-start(f32[2,4,128,64]{2,3,1,0:T(8,128)} %get-tuple-element.6) | copy-start | bytes 786436
  308.9 2.0 copy-start
Sparse Core Ops, SparseCore 0:
  22.3 268.3 all-reduce.2
where the time goes:
time: 340 us
  waiting for transfers between devices  268 us (79%)
  matrix products  39.7 us (12%)
  between operations  14.4 us (4%)
  local copies, waits for them, and re-layouts  11.4 us (3%)
  other arithmetic  6.28 us (2%)
    psum x1, waiting for transfers between devices, local(): lax.psum((jnp.stack(low_re_list), jnp.stack(low_im_list), jnp.stack(noise...  268 us
    dot_general x1, matrix products, finish_whole(): jnp.einsum('gtaij,hubji->gtahub', my_gammas, summed, precision=EXACT)  17.7 us
  transfers between devices with their start and end apart: 1, of which 1 were waited for; matrix products, arithmetic and copies ran while one was open for 0% of the time, Pallas kernels for 0%

commit v1 on v0

v1 whole, which is shorter than its diff:
```python
import functools

import jax
import jax.numpy as jnp
from jax import lax
from jax.experimental import pallas as pl
from jax.experimental.pallas import tpu as pltpu
from jax.sharding import PartitionSpec as P

AXES = ("gx", "gy", "gz")
EXACT = lax.Precision.HIGHEST
CHIPS = 128
ROWS = 20
VMEM = pltpu.MemorySpace.VMEM


def flat_index(chip, core):
    return (chip // 16) * 32 + core * 16 + chip % 16


CHIP_GROUPS = [[flat_index(chip, core) for chip in range(CHIPS)] for core in range(2)]
PARTNER = [(flat_index(chip, core), flat_index(chip, 1 - core)) for chip in range(CHIPS) for core in range(2)]


def lane_iota(shape):
    return lax.broadcasted_iota(jnp.int32, shape, len(shape) - 1)


def row_iota(shape):
    return lax.broadcasted_iota(jnp.int32, shape, len(shape) - 2)


def lane_swap(x, step):
    odd = (lane_iota(x.shape) & step) != 0
    return jnp.where(odd, pltpu.roll(x, step, 1), pltpu.roll(x, 128 - step, 1))


def lane_xor(x, amount, bits):
    for bit in bits:
        flip = ((amount >> bit) & 1) != 0
        x = jnp.where(flip, lane_swap(x, 1 << bit), x)
    return x


def products_kernel(slot_ref, left_ref, right_ref, pick_ref, out_ref, rows_ref):
    step = pl.program_id(0)

    @pl.when(step == 0)
    def _():
        for part in range(2):
            for colour in range(3):
                at = (part * 3 + colour) * 512
                noise = None
                for spin in range(4):
                    rows_ref[spin * 64 : spin * 64 + 64, at : at + 512] = right_ref[0, spin, part, colour, 0:64, :]
                    term = right_ref[0, spin, part, colour, 64:128, :] * pick_ref[spin]
                    noise = term if noise is None else noise + term
                rows_ref[256:320, at : at + 512] = noise

    cols = []
    for part in range(2):
        for colour in range(3):
            pieces = []
            for tile in range(2):
                lines = slice(tile * 16, tile * 16 + 16)
                for spin in range(4):
                    pieces.append(left_ref[0, spin, part, colour, lines, :])
                for spin in range(4):
                    other = left_ref[0, spin, 1 - part, colour, lines, :]
                    pieces.append(-other if part == 0 else other)
            cols.append(jnp.concatenate(pieces, axis=0))
    prod = lax.dot_general(
        rows_ref[...],
        jnp.concatenate(cols, axis=1),
        (((1,), (1,)), ((), ())),
        preferred_element_type=jnp.float32,
    )
    low_i = lane_iota((8, 128)) & 15
    within = row_iota((8, 128)) ^ (low_i & 7)
    upper = low_i >= 8
    for tile in range(2):
        i_high = step * 2 + tile
        for block in range(20):
            first = prod[block * 16 : block * 16 + 8, tile * 128 : tile * 128 + 128]
            second = prod[block * 16 + 8 : block * 16 + 16, tile * 128 : tile * 128 + 128]
            j_high = block % 4 if block < 16 else block - 12
            start = (i_high ^ j_high) * (16 * ROWS) + block
            low_half = jnp.take_along_axis(jnp.where(upper, second, first), within, axis=0)
            high_half = jnp.take_along_axis(jnp.where(upper, first, second), within, axis=0)
            out_ref[pl.ds(start, 8, stride=ROWS), :] = low_half
            out_ref[pl.ds(start + 8 * ROWS, 8, stride=ROWS), :] = high_half


def products(left, right, pick, slot):
    grid_spec = pltpu.PrefetchScalarGridSpec(
        num_scalar_prefetch=1,
        grid=(4,),
        in_specs=[
            pl.BlockSpec((1, 4, 2, 3, 32, 512), lambda n, slot: (slot[0], 0, 0, 0, n, 0)),
            pl.BlockSpec((1, 4, 2, 3, 128, 512), lambda n, slot: (slot[0], 0, 0, 0, 0, 0)),
            pl.BlockSpec((4, 64, 512), lambda n, slot: (0, 0, 0)),
        ],
        out_specs=pl.BlockSpec((CHIPS * ROWS, 128), lambda n, slot: (0, 0)),
        scratch_shapes=[pltpu.VMEM((320, 3072), jnp.bfloat16)],
    )
    return pl.pallas_call(
        products_kernel,
        grid_spec=grid_spec,
        out_shape=jax.ShapeDtypeStruct((CHIPS * ROWS, 128), jnp.float32),
        compiler_params=pltpu.CompilerParams(dimension_semantics=("arbitrary",)),
        name="products",
    )(slot, left, right, pick)


def sum_kernel(parts_ref, out_ref):
    def add(k, acc):
        return acc + parts_ref[pl.ds(pl.multiple_of(k * 40, 8), 40), :]

    both = lax.fori_loop(1, 64, add, parts_ref[0:40, :], unroll=7)
    out_ref[...] = both[0:20] + both[20:40]


def dot_exact(a, b, dims):
    return lax.dot_general(a, b, (dims, ((), ())), precision=EXACT, preferred_element_type=jnp.float32)


def combine_kernel(where_ref, own_ref, peer_ref, coef_ref, dil_ref, out_ref):
    chip = where_ref[0]
    core = where_ref[1]
    lane8 = lane_iota((8, 128))
    row8 = row_iota((8, 128))
    spin_of = lane_xor(dil_ref[...], chip & 15, range(4))
    noise_lane = lane8 >= 64
    fields = []
    for source in (own_ref, peer_ref):
        terms = []
        for spin in range(4):
            x = jnp.concatenate([source[spin * 4 : spin * 4 + 4, :], source[16:20, :]], axis=0)
            for level in range(3):
                row_bit = (row8 >> level) & 1
                lane_bit = (lane8 >> (level + 4)) & 1
                up = pltpu.roll(pltpu.roll(x, 1 << level, 0), 128 - (16 << level), 1)
                down = pltpu.roll(pltpu.roll(x, 8 - (1 << level), 0), 16 << level, 1)
                x = jnp.where(row_bit == lane_bit, x, jnp.where(row_bit == 1, up, down))
            keep = jnp.logical_or(jnp.logical_not(noise_lane), spin_of == spin)
            terms.append(jnp.where(keep, x, 0.0))
        fields.append(dot_exact(coef_ref[...], jnp.concatenate(terms, axis=0), ((1,), (0,))))
    mine, other = fields
    first = jnp.where(core == 0, mine, other)
    second = jnp.where(core == 0, other, mine)
    mirror = lane_xor(jnp.concatenate([first, second], axis=0), chip, range(7))
    cross = dot_exact(mine, mirror, ((1,), (1,)))
    zero = jnp.zeros((16, 64), jnp.float32)
    columns = []
    imag_columns = []
    for time in range(2):
        at = time * 32
        columns.append(cross[0:16, at : at + 16] - cross[16:32, at + 16 : at + 32])
        columns.append(cross[0:16, at + 16 : at + 32] + cross[16:32, at : at + 16])
    trace_rows = jnp.concatenate(columns + [zero], axis=1)
    ordered = lane_xor(mine, chip & 112, range(4, 7))
    lane = lane_iota((16, 128))
    for block in range(16):
        real = pltpu.roll(ordered[0:16], (64 - 8 * block) % 128, 1)
        imag = pltpu.roll(ordered[16:32], (72 - 8 * block) % 128, 1)
        rows = jnp.where(lane < 64, trace_rows, jnp.where(lane < 72, real, jnp.where(lane < 80, imag, 0.0)))
        out_ref[block * 16 : block * 16 + 16, :] = rows


def finish_kernel(where_ref, pairs_ref, got_ref, fields_ref, traces_ref):
    block = where_ref[2]
    lane = lane_iota((16, 128))
    row = row_iota((16, 128))
    sums = []
    for time in range(2):
        pieces = [got_ref[(k * 2 + time) * 16 : (k * 2 + time) * 16 + 16, :] for k in range(8)]
        total = pieces[0]
        for piece in pieces[1:]:
            total = total + piece
        sums.append(jnp.sum(total, axis=0, keepdims=True))
        by_chip = jnp.transpose(jnp.concatenate(pieces, axis=0))[64:80, :]
        x = lane_xor(by_chip, block * 8, range(3, 7))
        for bit in range(3):
            x = jnp.where(((row >> bit) & 1) != 0, lane_swap(x, 1 << bit), x)
        fields_ref[0, time, 0] = x[0:8]
        fields_ref[0, time, 1] = x[8:16]
    for pair in range(4):
        first = jnp.where(pairs_ref[pair, 0] == 0, sums[0], sums[1])
        picked = jnp.where(pairs_ref[pair, 1] == 0, first[:, 0:32], first[:, 32:64])
        traces_ref[pair : pair + 1, :] = picked / 128.0


def coefficients(gamma_cols, gamma_phase):
    spin_ids = jnp.arange(4, dtype=jnp.int32)
    onehot = (gamma_cols[:, :, None] == spin_ids[None, None, :]).astype(jnp.float32)
    real_sign = (gamma_phase == 0).astype(jnp.float32) - (gamma_phase == 2).astype(jnp.float32)
    imag_sign = (gamma_phase == 1).astype(jnp.float32) - (gamma_phase == 3).astype(jnp.float32)
    real = (onehot * real_sign[:, :, None]).transpose(0, 2, 1)
    imag = (onehot * imag_sign[:, :, None]).transpose(0, 2, 1)
    top = jnp.stack([real, -imag], axis=2)
    bottom = jnp.stack([imag, real], axis=2)
    return jnp.stack([top, bottom]).reshape(32, 32)


def whole(shape):
    return pl.BlockSpec(shape, lambda *_: (0,) * len(shape), memory_space=VMEM)


SMEM = pl.BlockSpec(memory_space=pltpu.MemorySpace.SMEM)


def local(left_modes, right_modes, gamma_cols, gamma_phase, dilution, time_pairs):
    gx, gy, gz = (lax.axis_index(name) for name in AXES)
    core = gy % 2
    chip = (gx * 2 + gy // 2) * 16 + gz
    where = jnp.stack([chip, core, gx * 4 + gy]).astype(jnp.int32)
    left = jnp.transpose(left_modes, (0, 1, 2, 4, 3, 5))
    right = jnp.transpose(right_modes, (0, 1, 2, 4, 3, 5))
    pick = (dilution[None, :] == jnp.arange(4, dtype=jnp.int32)[:, None]).astype(jnp.bfloat16)
    pick = jnp.broadcast_to(pick[:, :, None], (4, 64, 512))
    coef = coefficients(gamma_cols, gamma_phase)
    dil = jnp.broadcast_to(jnp.concatenate([dilution, dilution])[None, :], (8, 128))

    away = products(left, right, pick, (1 - core)[None].astype(jnp.int32))
    arrived = lax.ppermute(away, AXES, PARTNER)
    home = products(left, right, pick, core[None].astype(jnp.int32))
    partial = (home + arrived).reshape(CHIPS * 5, 4, 128)
    parts = lax.all_to_all(partial, AXES, 0, 0, axis_index_groups=CHIP_GROUPS, tiled=True)
    own = pl.pallas_call(
        sum_kernel,
        in_specs=[whole((CHIPS * ROWS, 128))],
        out_specs=whole((ROWS, 128)),
        out_shape=jax.ShapeDtypeStruct((ROWS, 128), jnp.float32),
        name="sum_parts",
    )(parts.reshape(CHIPS * ROWS, 128))
    peer = lax.ppermute(own, AXES, PARTNER)
    rows = pl.pallas_call(
        combine_kernel,
        in_specs=[SMEM, whole((ROWS, 128)), whole((ROWS, 128)), whole((32, 32)), whole((8, 128))],
        out_specs=whole((256, 128)),
        out_shape=jax.ShapeDtypeStruct((256, 128), jnp.float32),
        name="combine",
    )(where, own, peer, coef, dil)
    got = lax.all_to_all(rows, AXES, 0, 0, tiled=True)
    fields, traces = pl.pallas_call(
        finish_kernel,
        in_specs=[SMEM, SMEM, whole((256, 128))],
        out_specs=[whole((1, 2, 2, 8, 128)), whole((4, 32))],
        out_shape=[
            jax.ShapeDtypeStruct((1, 2, 2, 8, 128), jnp.float32),
            jax.ShapeDtypeStruct((4, 32), jnp.float32),
        ],
        name="finish",
    )(where, time_pairs, got)
    traces = traces.reshape(4, 1, 2, 16).transpose(0, 1, 3, 2)
    return (fields, traces)


def solution(mesh):
    return jax.shard_map(
        local,
        mesh=mesh,
        in_specs=(
            P(None, None, None, None, None, AXES),
            P(None, None, None, None, None, AXES),
            P(),
            P(),
            P(),
            P(),
        ),
        out_specs=(P("gz", None, None, ("gx", "gy"), None), P(None, "gz", None, None)),
        check_vma=False,
    )
```

time: 340 us -> 103 us (0.30)
  waiting for transfers between devices: 268 us -> 44.9 us
  matrix products: 39.7 us -> 0 us
  starting transfers between devices: 0.04 us -> 26.7 us
  Pallas kernels: 0 us -> 20.5 us
  between operations: 14.4 us -> 0.75 us
  local copies, waits for them, and re-layouts: 11.4 us -> 5.93 us
    psum x1 -> x0, waiting for transfers between devices: 268 us -> none  [local(): lax.psum((jnp.stack(low_re_list), jnp.stack(low_im_list), jnp.stack(noise...]
    all_to_all x0 -> x2, waiting for transfers between devices: none -> 44.9 us  [the longest x1 32.7 us: local(): lax.all_to_all(partial, AXES, 0, 0, axis_index_groups=CHIP_GROUPS, tiled=...]
    dot_general x16 -> x0, matrix products: 39.7 us -> none  [the longest x1 17.7 us: finish_whole(): jnp.einsum('gtaij,hubji->gtahub', my_gammas, summed, precision=EXACT)]
    all_to_all x0 -> x2, starting transfers between devices: none -> 21.5 us  [the longest x1 13.9 us: local(): lax.all_to_all(partial, AXES, 0, 0, axis_index_groups=CHIP_GROUPS, tiled=...]
    pallas_call x0 -> x5, Pallas kernels: none -> 20.5 us  [the longest x2 13.7 us: products(): pl.pallas_call(products_kernel, grid_spec=grid_spec, out_shape=jax.ShapeD...]
    ppermute x0 -> x2, starting transfers between devices: none -> 5.17 us  [the longest x1 3.21 us: local(): arrived = lax.ppermute(away, AXES, PARTNER)]
    squeeze x2 -> x0, local copies, waits for them, and re-layouts: 4.23 us -> none  [the longest x1 3.48 us: local(): right_slot = right_modes[time_slot]]
  transfers between devices with their start and end apart: 1 -> 4, of which waited for: 1 -> 2; matrix products, arithmetic and copies ran while one was open for 0% -> 2% of each run, Pallas kernels for 0% -> 7%
where the time goes in v1:
time: 103 us
  waiting for transfers between devices  44.9 us (44%)
  starting transfers between devices  26.7 us (26%)
  Pallas kernels  20.5 us (20%)
  local copies, waits for them, and re-layouts  5.93 us (6%)
  other arithmetic  3.98 us (4%)
    all_to_all x1, waiting for transfers between devices, local(): lax.all_to_all(partial, AXES, 0, 0, axis_index_groups=CHIP_GROUPS, tiled=...  32.7 us
    all_to_all x1, starting transfers between devices, local(): lax.all_to_all(partial, AXES, 0, 0, axis_index_groups=CHIP_GROUPS, tiled=...  13.9 us
    pallas_call x2, Pallas kernels, products(): pl.pallas_call(products_kernel, grid_spec=grid_spec, out_shape=jax.ShapeD...  13.7 us
    all_to_all x1, waiting for transfers between devices, local(): got = lax.all_to_all(rows, AXES, 0, 0, tiled=True)  12.2 us
    all_to_all x1, starting transfers between devices, local(): got = lax.all_to_all(rows, AXES, 0, 0, tiled=True)  7.56 us
    ppermute x1, starting transfers between devices, local(): arrived = lax.ppermute(away, AXES, PARTNER)  3.21 us
    pallas_call x1, Pallas kernels, local(): pl.pallas_call(combine_kernel, in_specs=[SMEM, whole((ROWS, 128)), whole(...  2.69 us
    add x1, other arithmetic, local(): partial = (home + arrived).reshape(CHIPS * 5, 4, 128)  2.52 us
  transfers between devices with their start and end apart: 4, of which 2 were waited for; matrix products, arithmetic and copies ran while one was open for 2% of the time, Pallas kernels for 7%

profile of v1, /device:TPU:1, one launch (start us, length us, event | category | flops | bytes accessed | tf_op | source)
XLA Modules:
  0.0 102.7 jit_solution(4658222241881637666)
XLA Ops:
  0.6 0.7 fusion.2
  1.3 0.8 broadcast_in_dim.6.pick_ref
  2.1 6.9 %products.3 = f32[2560,128]{1,0:T(8,128)} custom-call(s32[1]{0:T(128)} %bitcast.5.slot_ref, bf16[2,4,2,3,128,512]{5,4,3,2,1,0:T(8,128)(2,1)} %bitcast.21, bf16[2,4,2,3,128,512]{5,4,3,2,1,0:T(8,128)(2,1)} %bitcast.23, bf16[4,64,512]{2,1,0:T(8,128)(2,1)} %broadcast_in_dim.6.pick_ref), custom_call_target="tpu_custom_call" | custom-call | tf_op jit(solution)/shard_map/products/pallas_call | solution.py:106
  9.0 3.2 %collective-permute-start = (f32[2560,128]{1,0:T(8,128)}, f32[2560,128]{1,0:T(8,128)S(1)}, u32[]{:S(2)}, u32[]{:S(2)}) collective-permute-start(f32[2560,128]{1,0:T(8,128)} %products.3), channel_id=1, source_target_pairs={{0,16},{16,0},{1,17},{17,1},{2,18},{18,2},{3,19},{19,3},{4,20},{20... | collective-permute-start | bytes 3932168 | tf_op jit(solution)/shard_map/ppermute | solution.py:225
  12.2 6.9 %products.2 = f32[2560,128]{1,0:T(8,128)} custom-call(s32[1]{0:T(128)} %bitcast.1.slot_ref, bf16[2,4,2,3,128,512]{5,4,3,2,1,0:T(8,128)(2,1)} %bitcast.22, bf16[2,4,2,3,128,512]{5,4,3,2,1,0:T(8,128)(2,1)} %bitcast.24, bf16[4,64,512]{2,1,0:T(8,128)(2,1)} %broadcast_in_dim.6.pick_ref), custom_call_target="tpu_custom_call" | custom-call | tf_op jit(solution)/shard_map/products/pallas_call | solution.py:106
  19.1 2.5 %add.21 = f32[2560,128]{1,0:T(8,128)} add(f32[2560,128]{1,0:T(8,128)} %products.2, f32[2560,128]{1,0:T(8,128)S(1)} %collective-permute-done) | non-fusion elementwise | flops 327680 | bytes 3932160 | tf_op jit(solution)/shard_map/add | solution.py:227
  21.6 13.9 %all-to-all-start = ((f32[640,4,128]{2,1,0:T(4,128)}), f32[640,4,128]{2,1,0:T(4,128)S(1)}, u32[]{:S(2)}, u32[]{:S(2)}) async-start(f32[640,4,128]{2,1,0:T(4,128)} %bitcast.6), calls=%async_computation | async-start | bytes 2621440 | tf_op jit(solution)/shard_map/all_to_all | solution.py:228
  35.5 0.0 copy-start.5
  35.6 0.1 pad_add_fusion.1
  35.7 32.7 %all-to-all-done = f32[640,4,128]{2,1,0:T(4,128)S(1)} async-done(((f32[640,4,128]{2,1,0:T(4,128)}), f32[640,4,128]{2,1,0:T(4,128)S(1)}, u32[]{:S(2)}, u32[]{:S(2)}) %all-to-all-start) | async-done | bytes 1310752 | tf_op jit(solution)/shard_map/all_to_all | solution.py:228
  68.4 1.1 %copy-done = f32[640,4,128]{2,1,0:T(4,128)} copy-done((f32[640,4,128]{2,1,0:T(4,128)}, f32[640,4,128]{2,1,0:T(4,128)S(1)}, u32[]{:S(2)}) %copy-start) | copy-done | bytes 1310744
  69.5 2.0 %sum_parts.1.own_ref = f32[20,128]{1,0:T(8,128)} custom-call(f32[2560,128]{1,0:T(8,128)} %bitcast.25), custom_call_target="tpu_custom_call" | custom-call | tf_op jit(solution)/shard_map/sum_parts/pallas_call | solution.py:229
  71.5 2.0 %collective-permute-start.1 = (f32[20,128]{1,0:T(8,128)}, f32[20,128]{1,0:T(8,128)S(1)}, u32[]{:S(2)}, u32[]{:S(2)}) collective-permute-start(f32[20,128]{1,0:T(8,128)} %sum_parts.1.own_ref), channel_id=1, source_target_pairs={{0,16},{16,0},{1,17},{17,1},{2,18},{18,2},{3,19},{19,3},{4,20},{20... | collective-permute-start | bytes 30728 | tf_op jit(solution)/shard_map/ppermute | solution.py:236
  73.5 0.7 pad_add_fusion.where_ref
  74.1 0.1 reshape.58
  74.2 0.7 copy.18.coef_ref
  74.9 0.6 broadcast_in_dim.8.dil_ref
  75.5 2.7 %combine.1 = f32[256,128]{1,0:T(8,128)} custom-call(s32[3]{0:T(128)} %pad_add_fusion.where_ref, f32[20,128]{1,0:T(8,128)} %sum_parts.1.own_ref, f32[20,128]{1,0:T(8,128)} %copy-done.2, f32[32,32]{1,0:T(8,128)} %copy.18.coef_ref, s32[8,128]{1,0:T(8,128)} %broadcast_in_dim.8.dil_ref), custom_call_target="tpu_custom_call" | custom-call | tf_op jit(solution)/shard_map/combine/pallas_call | solution.py:237
  78.2 7.6 %all-to-all-start.1 = ((f32[256,1,128]{2,1,0:T(1,128)}), f32[256,1,128]{2,1,0:T(1,128)S(1)}, u32[]{:S(2)}, u32[]{:S(2)}) async-start(f32[256,1,128]{2,1,0:T(1,128)} %bitcast.27), calls=%async_computation.1 | async-start | bytes 262144 | tf_op jit(solution)/shard_map/all_to_all | solution.py:244
  85.8 0.7 copy.20.pairs_ref
  86.4 12.2 %all-to-all-done.1 = f32[256,1,128]{2,1,0:T(1,128)S(1)} async-done(((f32[256,1,128]{2,1,0:T(1,128)}), f32[256,1,128]{2,1,0:T(1,128)S(1)}, u32[]{:S(2)}, u32[]{:S(2)}) %all-to-all-start.1) | async-done | bytes 131104 | tf_op jit(solution)/shard_map/all_to_all | solution.py:244
  98.7 0.7 copy-done.1
  99.3 2.1 %finish.1 = (f32[1,2,2,8,128]{4,3,2,1,0:T(8,128)}, f32[4,32]{1,0:T(4,128)}) custom-call(s32[3]{0:T(128)} %pad_add_fusion.where_ref, s32[4,2]{1,0:T(4,128)} %copy.20.pairs_ref, f32[256,128]{1,0:T(8,128)} %bitcast.26), custom_call_target="tpu_custom_call" | custom-call | tf_op jit(solution)/shard_map/finish/pallas_call | solution.py:245
  101.4 1.3 %reshape.59 = f32[4,1,2,16]{3,2,0,1:T(2,128)} reshape(f32[4,32]{1,0:T(4,128)} %get-tuple-element.5) | data formatting | bytes 1024 | tf_op jit(solution)/shard_map/reshape | solution.py:255
  (17 shorter events, 0.1 us)
Async XLA Ops:
  9.0 10.1 %collective-permute-start = (f32[2560,128]{1,0:T(8,128)}, f32[2560,128]{1,0:T(8,128)S(1)}, u32[]{:S(2)}, u32[]{:S(2)}) collective-permute-start(f32[2560,128]{1,0:T(8,128)} %products.3), channel_id=1, source_target_pairs={{0,16},{16,0},{1,17},{17,1},{2,18},{18,2},{3,19},{19,3},{4,20},{20... | collective-permute-start | bytes 3932168 | tf_op jit(solution)/shard_map/ppermute | solution.py:225
  21.6 14.0 %copy-start.6 = (s32[64]{0:T(128)S(1)}, s32[64]{0:T(128)}, u32[]{:S(2)}) copy-start(s32[64]{0:T(128)} %param.10) | copy-start | bytes 772
  21.6 14.1 %copy-start.3 = (s32[16,4]{0,1:T(4,128)S(1)}, s32[16,4]{0,1:T(4,128)}, u32[]{:S(2)}) copy-start(s32[16,4]{0,1:T(4,128)} %param.9) | copy-start | bytes 772
  21.6 14.1 %copy-start.4 = (s32[16,4]{0,1:T(4,128)S(1)}, s32[16,4]{0,1:T(4,128)}, u32[]{:S(2)}) copy-start(s32[16,4]{0,1:T(4,128)} %param.8) | copy-start | bytes 772
  21.6 46.8 %all-to-all-start = ((f32[640,4,128]{2,1,0:T(4,128)}), f32[640,4,128]{2,1,0:T(4,128)S(1)}, u32[]{:S(2)}, u32[]{:S(2)}) async-start(f32[640,4,128]{2,1,0:T(4,128)} %bitcast.6), calls=%async_computation | async-start | bytes 2621440 | tf_op jit(solution)/shard_map/all_to_all | solution.py:228
  35.5 50.2 %copy-start.5 = (s32[4,2]{0,1:T(2,128)S(1)}, s32[4,2]{0,1:T(2,128)}, u32[]{:S(2)}) copy-start(s32[4,2]{0,1:T(2,128)} %param.11) | copy-start | bytes 100
  68.4 1.1 %copy-start = (f32[640,4,128]{2,1,0:T(4,128)}, f32[640,4,128]{2,1,0:T(4,128)S(1)}, u32[]{:S(2)}) copy-start(f32[640,4,128]{2,1,0:T(4,128)S(1)} %all-to-all-done) | copy-start | bytes 3932164
  71.5 3.4 %collective-permute-start.1 = (f32[20,128]{1,0:T(8,128)}, f32[20,128]{1,0:T(8,128)S(1)}, u32[]{:S(2)}, u32[]{:S(2)}) collective-permute-start(f32[20,128]{1,0:T(8,128)} %sum_parts.1.own_ref), channel_id=1, source_target_pairs={{0,16},{16,0},{1,17},{17,1},{2,18},{18,2},{3,19},{19,3},{4,20},{20... | collective-permute-start | bytes 30728 | tf_op jit(solution)/shard_map/ppermute | solution.py:236
  74.9 0.6 copy-start.2
  78.2 20.5 %all-to-all-start.1 = ((f32[256,1,128]{2,1,0:T(1,128)}), f32[256,1,128]{2,1,0:T(1,128)S(1)}, u32[]{:S(2)}, u32[]{:S(2)}) async-start(f32[256,1,128]{2,1,0:T(1,128)} %bitcast.27), calls=%async_computation.1 | async-start | bytes 262144 | tf_op jit(solution)/shard_map/all_to_all | solution.py:244
  98.7 0.7 copy-start.1

commit v2 on v1

v2 whole, which is shorter than its diff:
```python
import jax
import jax.numpy as jnp
from jax import lax
from jax.experimental import pallas as pl
from jax.experimental.pallas import tpu as pltpu
from jax.sharding import PartitionSpec as P

AXES = ("gx", "gy", "gz")
EXACT = lax.Precision.HIGHEST
CHIPS = 128
ROWS = 20
VMEM = pltpu.MemorySpace.VMEM


def flat_index(chip, core):
    return (chip // 16) * 32 + core * 16 + (chip % 8) * 2 + (chip // 8) % 2


PLANES = [[flat_index(plane * 8 + z, core) for plane in range(16)] for z in range(8) for core in range(2)]
COLUMNS = [[flat_index(plane * 8 + z, core) for z in range(8)] for plane in range(16) for core in range(2)]
PARTNER = [(flat_index(chip, core), flat_index(chip, 1 - core)) for chip in range(CHIPS) for core in range(2)]


def lane_iota(shape):
    return lax.broadcasted_iota(jnp.int32, shape, len(shape) - 1)


def row_iota(shape):
    return lax.broadcasted_iota(jnp.int32, shape, len(shape) - 2)


def lane_swap(x, step):
    odd = (lane_iota(x.shape) & step) != 0
    return jnp.where(odd, pltpu.roll(x, step, 1), pltpu.roll(x, 128 - step, 1))


def lane_xor(x, amount, bits):
    for bit in bits:
        flip = ((amount >> bit) & 1) != 0
        x = jnp.where(flip, lane_swap(x, 1 << bit), x)
    return x


def products_kernel(slot_ref, left_ref, right_ref, dil_ref, out_ref, rows_ref):
    step = pl.program_id(0)

    @pl.when(step == 0)
    def _():
        dilution = jnp.broadcast_to(jnp.concatenate([dil_ref[...], dil_ref[...]], axis=1), (128, 128))
        spin_of = jnp.transpose(dilution)[0:64, :]
        pick = []
        for spin in range(4):
            one = jnp.where(spin_of == spin, 1.0, 0.0).astype(jnp.bfloat16)
            pick.append(jnp.concatenate([one] * 4, axis=1))
        for part in range(2):
            for colour in range(3):
                at = (part * 3 + colour) * 512
                noise = None
                for spin in range(4):
                    rows_ref[spin * 64 : spin * 64 + 64, at : at + 512] = right_ref[0, spin, part, colour, 0:64, :]
                    term = right_ref[0, spin, part, colour, 64:128, :] * pick[spin]
                    noise = term if noise is None else noise + term
                rows_ref[256:320, at : at + 512] = noise

    cols = []
    for part in range(2):
        for colour in range(3):
            pieces = []
            for tile in range(2):
                lines = slice(tile * 16, tile * 16 + 16)
                for spin in range(4):
                    pieces.append(left_ref[0, spin, part, colour, lines, :])
                for spin in range(4):
                    other = left_ref[0, spin, 1 - part, colour, lines, :]
                    pieces.append(-other if part == 0 else other)
            cols.append(jnp.concatenate(pieces, axis=0))
    prod = lax.dot_general(
        rows_ref[...],
        jnp.concatenate(cols, axis=1),
        (((1,), (1,)), ((), ())),
        preferred_element_type=jnp.float32,
    )
    low_i = lane_iota((8, 128)) & 15
    within = row_iota((8, 128)) ^ (low_i & 7)
    upper = low_i >= 8
    for tile in range(2):
        i_high = step * 2 + tile
        for block in range(20):
            first = prod[block * 16 : block * 16 + 8, tile * 128 : tile * 128 + 128]
            second = prod[block * 16 + 8 : block * 16 + 16, tile * 128 : tile * 128 + 128]
            j_high = block % 4 if block < 16 else block - 12
            start = (i_high ^ j_high) * (16 * ROWS) + block
            low_half = jnp.take_along_axis(jnp.where(upper, second, first), within, axis=0)
            high_half = jnp.take_along_axis(jnp.where(upper, first, second), within, axis=0)
            out_ref[pl.ds(start, 8, stride=ROWS), :] = low_half
            out_ref[pl.ds(start + 8 * ROWS, 8, stride=ROWS), :] = high_half


def products(left, right, dil, slot):
    grid_spec = pltpu.PrefetchScalarGridSpec(
        num_scalar_prefetch=1,
        grid=(4,),
        in_specs=[
            pl.BlockSpec((1, 4, 2, 3, 32, 512), lambda n, slot: (slot[0], 0, 0, 0, n, 0)),
            pl.BlockSpec((1, 4, 2, 3, 128, 512), lambda n, slot: (slot[0], 0, 0, 0, 0, 0)),
            pl.BlockSpec((1, 64), lambda n, slot: (0, 0)),
        ],
        out_specs=pl.BlockSpec(memory_space=VMEM),
        scratch_shapes=[pltpu.VMEM((320, 3072), jnp.bfloat16)],
    )
    return pl.pallas_call(
        products_kernel,
        grid_spec=grid_spec,
        out_shape=pltpu.VMEM((CHIPS * ROWS, 128), jnp.float32),
        compiler_params=pltpu.CompilerParams(dimension_semantics=("arbitrary",)),
        name="products",
    )(slot, left, right, dil)


def place():
    gx, gy, gz = (lax.axis_index(name) for name in AXES)
    chip = gx * 32 + (gy >> 1) * 16 + (gz & 1) * 8 + (gz >> 1)
    return chip, gy & 1, gx * 4 + gy


def sum_planes_kernel(parts_ref, out_ref):
    total = parts_ref[0:160, :]
    for k in range(1, 16):
        total = total + parts_ref[k * 160 : k * 160 + 160, :]
    out_ref[...] = total


def sum_columns_kernel(parts_ref, out_ref):
    both = parts_ref[0:40, :]
    for k in range(1, 4):
        both = both + parts_ref[k * 40 : k * 40 + 40, :]
    out_ref[...] = both[0:20] + both[20:40]


def dot_exact(a, b, dims):
    return lax.dot_general(a, b, (dims, ((), ())), precision=EXACT, preferred_element_type=jnp.float32)


def combine_kernel(own_ref, peer_ref, cols_ref, phase_ref, dil_ref, out_ref):
    chip, core, _ = place()
    coef = coefficients(cols_ref[...], phase_ref[...])
    lane8 = lane_iota((8, 128))
    row8 = row_iota((8, 128))
    dilution = jnp.broadcast_to(jnp.concatenate([dil_ref[...], dil_ref[...]], axis=1), (8, 128))
    spin_of = lane_xor(dilution, chip & 15, range(4))
    noise_lane = lane8 >= 64
    fields = []
    for source in (own_ref, peer_ref):
        terms = []
        for spin in range(4):
            x = jnp.concatenate([source[spin * 4 : spin * 4 + 4, :], source[16:20, :]], axis=0)
            for level in range(3):
                row_bit = (row8 >> level) & 1
                lane_bit = (lane8 >> (level + 4)) & 1
                up = pltpu.roll(pltpu.roll(x, 1 << level, 0), 128 - (16 << level), 1)
                down = pltpu.roll(pltpu.roll(x, 8 - (1 << level), 0), 16 << level, 1)
                x = jnp.where(row_bit == lane_bit, x, jnp.where(row_bit == 1, up, down))
            keep = jnp.logical_or(jnp.logical_not(noise_lane), spin_of == spin)
            terms.append(jnp.where(keep, x, 0.0))
        fields.append(dot_exact(coef, jnp.concatenate(terms, axis=0), ((0,), (0,))))
    mine, other = fields
    first = jnp.where(core == 0, mine, other)
    second = jnp.where(core == 0, other, mine)
    mirror = lane_xor(jnp.concatenate([first, second], axis=0), chip, range(7))
    cross = dot_exact(mine, mirror, ((1,), (1,)))
    zero = jnp.zeros((16, 64), jnp.float32)
    columns = []
    imag_columns = []
    for time in range(2):
        at = time * 32
        columns.append(cross[0:16, at : at + 16] - cross[16:32, at + 16 : at + 32])
        columns.append(cross[0:16, at + 16 : at + 32] + cross[16:32, at : at + 16])
    trace_rows = jnp.concatenate(columns + [zero], axis=1)
    ordered = lane_xor(mine, chip & 112, range(4, 7))
    lane = lane_iota((16, 128))
    for block in range(16):
        real = pltpu.roll(ordered[0:16], (64 - 8 * block) % 128, 1)
        imag = pltpu.roll(ordered[16:32], (72 - 8 * block) % 128, 1)
        rows = jnp.where(lane < 64, trace_rows, jnp.where(lane < 72, real, jnp.where(lane < 80, imag, 0.0)))
        out_ref[block * 16 : block * 16 + 16, :] = rows


def finish_kernel(pairs_ref, got_ref, fields_ref, traces_ref):
    _, _, block = place()
    row = row_iota((16, 128))
    sums = []
    for time in range(2):
        pieces = []
        for k in range(8):
            for high in range(2):
                pieces.append(got_ref[pl.ds((k * 2 + time) * 16 + high, 8, stride=2), :])
        total = pieces[0]
        for piece in pieces[1:]:
            total = total + piece
        sums.append(jnp.sum(total, axis=0, keepdims=True))
        by_chip = jnp.transpose(jnp.concatenate(pieces, axis=0))[64:80, :]
        x = lane_xor(by_chip, block * 8, range(3, 7))
        for bit in range(3):
            x = jnp.where(((row >> bit) & 1) != 0, lane_swap(x, 1 << bit), x)
        fields_ref[0, time, 0] = x[0:8]
        fields_ref[0, time, 1] = x[8:16]
    for pair in range(4):
        first = jnp.where(pairs_ref[pair, 0] == 0, sums[0], sums[1])
        picked = jnp.where(pairs_ref[pair, 1] == 0, first[:, 0:32], first[:, 32:64]) / 128.0
        traces_ref[pair, 0, 0:1, :] = picked[:, 0:16]
        traces_ref[pair, 0, 1:2, :] = picked[:, 16:32]


def coefficients(cols, phase):
    real = jnp.where(phase == 0, 1.0, jnp.where(phase == 2, -1.0, 0.0))
    imag = jnp.where(phase == 1, 1.0, jnp.where(phase == 3, -1.0, 0.0))
    blocks = []
    for spin in range(4):
        here = jnp.where(cols == spin, 1.0, 0.0)
        blocks.append(jnp.concatenate([here * real, here * imag], axis=1))
        blocks.append(jnp.concatenate([-here * imag, here * real], axis=1))
    return jnp.concatenate(blocks, axis=0)


def in_vmem(x):
    return pltpu.with_memory_space_constraint(x, VMEM)


VMEM_SPEC = pl.BlockSpec(memory_space=VMEM)
SMEM_SPEC = pl.BlockSpec(memory_space=pltpu.MemorySpace.SMEM)


def call(kernel, name, out_shape, *operands, specs=None):
    return pl.pallas_call(
        kernel,
        in_specs=specs or [VMEM_SPEC] * len(operands),
        out_specs=jax.tree.map(lambda _: VMEM_SPEC, out_shape),
        out_shape=out_shape,
        name=name,
    )(*operands)


def local(left_modes, right_modes, gamma_cols, gamma_phase, dilution, time_pairs):
    core = lax.axis_index("gy") % 2
    left = jnp.transpose(left_modes, (0, 1, 2, 4, 3, 5))
    right = jnp.transpose(right_modes, (0, 1, 2, 4, 3, 5))
    dil = dilution.reshape(1, 64)

    away = products(left, right, dil, (1 - core)[None].astype(jnp.int32))
    arrived = lax.ppermute(away, AXES, PARTNER)
    home = products(left, right, dil, core[None].astype(jnp.int32))
    partial = (home + arrived).reshape(16, 160, 128)
    parts = lax.all_to_all(partial, AXES, 0, 0, axis_index_groups=PLANES, tiled=True)
    plane = call(sum_planes_kernel, "sum_planes", pltpu.VMEM((160, 128), jnp.float32), in_vmem(parts.reshape(2560, 128)))
    parts = lax.all_to_all(plane.reshape(8, 1, 2560), AXES, 0, 0, axis_index_groups=COLUMNS, tiled=True)
    own = call(sum_columns_kernel, "sum_columns", pltpu.VMEM((ROWS, 128), jnp.float32), in_vmem(parts.reshape(160, 128)))
    peer = lax.ppermute(own, AXES, PARTNER)
    rows = call(
        combine_kernel,
        "combine",
        pltpu.VMEM((256, 128), jnp.float32),
        in_vmem(own),
        in_vmem(peer),
        in_vmem(gamma_cols.T),
        in_vmem(gamma_phase.T),
        in_vmem(dil),
    )
    got = lax.all_to_all(rows.reshape(256, 1, 128), AXES, 0, 0, tiled=True)
    fields, traces = pl.pallas_call(
        finish_kernel,
        in_specs=[SMEM_SPEC, VMEM_SPEC],
        out_specs=[VMEM_SPEC, VMEM_SPEC],
        out_shape=[
            jax.ShapeDtypeStruct((1, 2, 2, 8, 128), jnp.float32),
            jax.ShapeDtypeStruct((4, 1, 2, 16), jnp.float32),
        ],
        name="finish",
    )(time_pairs, in_vmem(got.reshape(256, 128)))
    return (fields, jnp.swapaxes(traces, 2, 3))


def solution(mesh):
    return jax.shard_map(
        local,
        mesh=mesh,
        in_specs=(
            P(None, None, None, None, None, AXES),
            P(None, None, None, None, None, AXES),
            P(),
            P(),
            P(),
            P(),
        ),
        out_specs=(P("gz", None, None, ("gx", "gy"), None), P(None, "gz", None, None)),
        check_vma=False,
    )
```

time: 103 us -> 83.4 us (0.81)
  blocking collectives: 0 us -> 39.7 us
  waiting for transfers between devices: 44.9 us -> 13.2 us
  starting transfers between devices: 26.7 us -> 11.7 us
  local copies, waits for them, and re-layouts: 5.93 us -> 0.68 us
  Pallas kernels: 20.5 us -> 15.7 us
  other arithmetic: 3.98 us -> 1.45 us
    all_to_all x0 -> x2, blocking collectives: none -> 39.7 us  [the longest x1 24.2 us: local(): lax.all_to_all(partial, AXES, 0, 0, axis_index_groups=PLANES, tiled=True)]
    all_to_all x2 -> x1, waiting for transfers between devices: 44.9 us -> 12.4 us  [local(): got = lax.all_to_all(rows.reshape(256, 1, 128), AXES, 0, 0, tiled=True)]
    all_to_all x2 -> x1, starting transfers between devices: 21.5 us -> 5.36 us  [local(): got = lax.all_to_all(rows.reshape(256, 1, 128), AXES, 0, 0, tiled=True)]
    pallas_call x5 -> x6, Pallas kernels: 20.5 us -> 15.7 us  [the longest x2 11.7 us: products(): pl.pallas_call(products_kernel, grid_spec=grid_spec, out_shape=pltpu.VMEM...]
    reshape x3 -> x0, local copies, waits for them, and re-layouts: 2.09 us -> none  [the longest x1 1.33 us: local(): traces = traces.reshape(4, 1, 2, 16).transpose(0, 1, 3, 2)]
    unnamed x15 -> x9, local copies, waits for them, and re-layouts: 2.41 us -> 0.68 us
    broadcast_in_dim x2 -> x0, local copies, waits for them, and re-layouts: 1.43 us -> none  [the longest x1 0.83 us: local(): pick = jnp.broadcast_to(pick[:, :, None], (4, 64, 512))]
    ppermute x1, starting transfers between devices: 1.97 us -> 3.04 us  [local(): peer = lax.ppermute(own, AXES, PARTNER)]
  transfers between devices with their start and end apart: 4 -> 3, of which waited for: 2 -> 2; matrix products, arithmetic and copies ran while one was open for 2% -> 1% of each run, Pallas kernels for 7% -> 7%
where the time goes in v2:
time: 83.4 us; the launch traced here: 83.1 us
  blocking collectives  39.7 us (48%)
  Pallas kernels  15.7 us (19%)
  waiting for transfers between devices  13.2 us (16%)
  starting transfers between devices  11.7 us (14%)
  other arithmetic  1.45 us (2%)
    all_to_all x1, blocking collectives, local(): lax.all_to_all(partial, AXES, 0, 0, axis_index_groups=PLANES, tiled=True)  24.2 us
    all_to_all x1, blocking collectives, local(): lax.all_to_all(plane.reshape(8, 1, 2560), AXES, 0, 0, axis_index_groups=C...  15.5 us
    all_to_all x1, waiting for transfers between devices, local(): got = lax.all_to_all(rows.reshape(256, 1, 128), AXES, 0, 0, tiled=True)  12.4 us
    pallas_call x2, Pallas kernels, products(): pl.pallas_call(products_kernel, grid_spec=grid_spec, out_shape=pltpu.VMEM...  11.7 us
    all_to_all x1, starting transfers between devices, local(): got = lax.all_to_all(rows.reshape(256, 1, 128), AXES, 0, 0, tiled=True)  5.36 us
    ppermute x1, starting transfers between devices, local(): arrived = lax.ppermute(away, AXES, PARTNER)  3.29 us
    ppermute x1, starting transfers between devices, local(): peer = lax.ppermute(own, AXES, PARTNER)  3.04 us
    pallas_call x3, Pallas kernels, call(): pl.pallas_call(kernel, in_specs=specs or [VMEM_SPEC] * len(operands), out...  2.07 us
  transfers between devices with their start and end apart: 3, of which 2 were waited for; matrix products, arithmetic and copies ran while one was open for 1% of the time, Pallas kernels for 7%

profile of v2, /device:TPU:1, one launch (start us, length us, event | category | flops | bytes accessed | tf_op | source)
XLA Modules:
  0.0 83.1 jit_solution(6173135441936320988)
XLA Ops:
  0.6 5.9 %products.3 = f32[2560,128]{1,0:T(8,128)S(1)} custom-call(s32[1]{0:T(128)} %bitcast.4.slot_ref, bf16[2,4,2,3,128,512]{5,4,3,2,1,0:T(8,128)(2,1)} %bitcast.25, bf16[2,4,2,3,128,512]{5,4,3,2,1,0:T(8,128)(2,1)} %bitcast.27, s32[1,64]{1,0:T(1,128)} %bitcast.20), custom_call_target="tpu_custom_call" | custom-call | tf_op jit(solution)/shard_map/products/pallas_call | solution.py:111
  6.5 3.3 %collective-permute-start = (f32[2560,128]{1,0:T(8,128)S(1)}, f32[2560,128]{1,0:T(8,128)}, u32[]{:S(2)}, u32[]{:S(2)}) collective-permute-start(f32[2560,128]{1,0:T(8,128)S(1)} %products.3), channel_id=1, source_target_pairs={{0,16},{16,0},{2,18},{18,2},{4,20},{20,4},{6,22},{22,6},{8,24},{24... | collective-permute-start | bytes 3932168 | tf_op jit(solution)/shard_map/ppermute | solution.py:250
  9.8 5.8 %products.2 = f32[2560,128]{1,0:T(8,128)S(1)} custom-call(s32[1]{0:T(128)} %bitcast.slot_ref, bf16[2,4,2,3,128,512]{5,4,3,2,1,0:T(8,128)(2,1)} %bitcast.26, bf16[2,4,2,3,128,512]{5,4,3,2,1,0:T(8,128)(2,1)} %bitcast.28, s32[1,64]{1,0:T(1,128)} %bitcast.21), custom_call_target="tpu_custom_call" | custom-call | tf_op jit(solution)/shard_map/products/pallas_call | solution.py:111
  15.7 0.0 collective-permute-done
  15.7 1.5 %add.8 = f32[2560,128]{1,0:T(8,128)S(1)} add(f32[2560,128]{1,0:T(8,128)S(1)} %products.2, f32[2560,128]{1,0:T(8,128)} %collective-permute-done) | non-fusion elementwise | flops 327680 | bytes 3932160 | tf_op jit(solution)/shard_map/add | solution.py:252
  17.1 24.2 %all_to_all.15 = f32[16,160,128]{2,1,0:T(8,128)S(1)} all-to-all(f32[16,160,128]{2,1,0:T(8,128)S(1)} %bitcast.29), channel_id=1, replica_groups={{0,1,32,33,64,65,96,97,128,129,160,161,192,193,224,225},{16,17,48,49,80..., dimensions={0} | all-to-all | bytes 2621440 | tf_op jit(solution)/shard_map/all_to_all | solution.py:253
  41.4 0.0 copy-start
  41.4 0.0 copy-start.1
  41.4 0.0 copy-start.2
  41.4 0.0 copy-start.3
  41.4 0.1 sum_planes.1
  41.4 15.5 %all_to_all.16 = f32[8,1,2560]{2,1,0:T(1,128)S(1)} all-to-all(f32[8,1,2560]{2,1,0:T(1,128)S(1)} %bitcast.19), channel_id=1, replica_groups={{0,2,4,6,8,10,12,14},{16,18,20,22,24,26,28,30},{1,3,5,7,9,11,13,15},{17..., dimensions={0} | all-to-all | bytes 163840 | tf_op jit(solution)/shard_map/all_to_all | solution.py:255
  56.9 3.0 %collective-permute-start.1 = (f32[20,128]{1,0:T(8,128)S(1)}, f32[20,128]{1,0:T(8,128)S(1)}, u32[]{:S(2)}, u32[]{:S(2)}) collective-permute-start(f32[20,128]{1,0:T(8,128)S(1)} %sum_columns.1.own_ref), channel_id=1, source_target_pairs={{0,16},{16,0},{2,18},{18,2},{4,20},{20,4},{6,22},{22,6},{8,24},{24... | collective-permute-start | bytes 30728 | tf_op jit(solution)/shard_map/ppermute | solution.py:257
  60.0 0.8 %collective-permute-done.1.peer_ref = f32[20,128]{1,0:T(8,128)S(1)} collective-permute-done((f32[20,128]{1,0:T(8,128)S(1)}, f32[20,128]{1,0:T(8,128)S(1)}, u32[]{:S(2)}, u32[]{:S(2)}) %collective-permute-start.1) | collective-permute-done | bytes 10272 | tf_op jit(solution)/shard_map/ppermute | solution.py:257
  60.8 0.0 copy-done
  60.8 0.0 copy-done.1
  60.8 0.0 copy-done.2
  60.8 2.0 %combine.1 = f32[256,128]{1,0:T(8,128)} custom-call(f32[20,128]{1,0:T(8,128)S(1)} %sum_columns.1.own_ref, f32[20,128]{1,0:T(8,128)S(1)} %collective-permute-done.1.peer_ref, s32[4,16]{1,0:T(4,128)S(1)} %bitcast.23, s32[4,16]{1,0:T(4,128)S(1)} %bitcast.24, s32[1,64]{1,0:T(1,128)S(1)} %bitcast.22), custom_call_target="tpu_custom_call" | custom-call | tf_op jit(solution)/shard_map/combine/pallas_call | solution.py:234
  62.8 5.4 %all-to-all-start.2 = ((f32[256,1,128]{2,1,0:T(1,128)}), f32[256,1,128]{2,1,0:T(1,128)S(1)}, u32[]{:S(2)}, u32[]{:S(2)}) async-start(f32[256,1,128]{2,1,0:T(1,128)} %bitcast.12), calls=%async_computation.2 | async-start | bytes 262144 | tf_op jit(solution)/shard_map/all_to_all | solution.py:268
  68.2 0.0 copy-done.3
  68.2 0.7 copy.11.pairs_ref
  68.9 12.4 %all-to-all-done.2 = f32[256,1,128]{2,1,0:T(1,128)S(1)} async-done(((f32[256,1,128]{2,1,0:T(1,128)}), f32[256,1,128]{2,1,0:T(1,128)S(1)}, u32[]{:S(2)}, u32[]{:S(2)}) %all-to-all-start.2) | async-done | bytes 131104 | tf_op jit(solution)/shard_map/all_to_all | solution.py:268
  81.2 1.9 %finish.1 = (f32[1,2,2,8,128]{4,3,2,1,0:T(8,128)}, f32[4,1,2,16]{3,2,1,0:T(2,128)}) custom-call(s32[4,2]{1,0:T(4,128)} %copy.11.pairs_ref, f32[256,128]{1,0:T(8,128)S(1)} %bitcast.17), custom_call_target="tpu_custom_call" | custom-call | tf_op jit(solution)/shard_map/finish/pallas_call | solution.py:269
  (1 shorter events, 0.0 us)
Async XLA Ops:
  6.5 9.1 %collective-permute-start = (f32[2560,128]{1,0:T(8,128)S(1)}, f32[2560,128]{1,0:T(8,128)}, u32[]{:S(2)}, u32[]{:S(2)}) collective-permute-start(f32[2560,128]{1,0:T(8,128)S(1)} %products.3), channel_id=1, source_target_pairs={{0,16},{16,0},{2,18},{18,2},{4,20},{20,4},{6,22},{22,6},{8,24},{24... | collective-permute-start | bytes 3932168 | tf_op jit(solution)/shard_map/ppermute | solution.py:250
  41.4 19.5 %copy-start = (s32[64]{0:T(128)S(1)}, s32[64]{0:T(128)}, u32[]{:S(2)}) copy-start(s32[64]{0:T(128)} %param.10) | copy-start | bytes 772
  41.4 19.5 %copy-start.1 = (s32[16,4]{0,1:T(4,128)S(1)}, s32[16,4]{0,1:T(4,128)}, u32[]{:S(2)}) copy-start(s32[16,4]{0,1:T(4,128)} %param.8) | copy-start | bytes 772
  41.4 19.5 %copy-start.2 = (s32[16,4]{0,1:T(4,128)S(1)}, s32[16,4]{0,1:T(4,128)}, u32[]{:S(2)}) copy-start(s32[16,4]{0,1:T(4,128)} %param.9) | copy-start | bytes 772
  41.4 26.8 %copy-start.3 = (s32[4,2]{0,1:T(2,128)S(1)}, s32[4,2]{0,1:T(2,128)}, u32[]{:S(2)}) copy-start(s32[4,2]{0,1:T(2,128)} %param.11) | copy-start | bytes 100
  56.9 3.9 %collective-permute-start.1 = (f32[20,128]{1,0:T(8,128)S(1)}, f32[20,128]{1,0:T(8,128)S(1)}, u32[]{:S(2)}, u32[]{:S(2)}) collective-permute-start(f32[20,128]{1,0:T(8,128)S(1)} %sum_columns.1.own_ref), channel_id=1, source_target_pairs={{0,16},{16,0},{2,18},{18,2},{4,20},{20,4},{6,22},{22,6},{8,24},{24... | collective-permute-start | bytes 30728 | tf_op jit(solution)/shard_map/ppermute | solution.py:257
  62.8 18.4 %all-to-all-start.2 = ((f32[256,1,128]{2,1,0:T(1,128)}), f32[256,1,128]{2,1,0:T(1,128)S(1)}, u32[]{:S(2)}, u32[]{:S(2)}) async-start(f32[256,1,128]{2,1,0:T(1,128)} %bitcast.12), calls=%async_computation.2 | async-start | bytes 262144 | tf_op jit(solution)/shard_map/all_to_all | solution.py:268

commit v3 on v2

v3 whole, which is shorter than its diff:
```python
import jax
import jax.numpy as jnp
from jax import lax
from jax.experimental import pallas as pl
from jax.experimental.pallas import tpu as pltpu
from jax.sharding import PartitionSpec as P

AXES = ("gx", "gy", "gz")
EXACT = lax.Precision.HIGHEST
CHIPS = 128
ROWS = 20
VMEM = pltpu.MemorySpace.VMEM


def flat_index(chip, core):
    bit = [(chip >> k) & 1 for k in range(7)]
    return bit[6] * 128 + bit[4] * 64 + bit[3] * 32 + core * 16 + (chip % 8) * 2 + bit[5]


PLANES = [[flat_index(plane * 8 + z, core) for plane in range(16)] for z in range(8) for core in range(2)]
COLUMNS = [[flat_index(plane * 8 + z, core) for z in range(8) for core in range(2)] for plane in range(16)]
PARTNER = [(flat_index(chip, core), flat_index(chip, 1 - core)) for chip in range(CHIPS) for core in range(2)]
SAME_CORE = [sorted(flat_index(chip, core) for chip in range(CHIPS)) for core in range(2)]


def lane_iota(shape):
    return lax.broadcasted_iota(jnp.int32, shape, len(shape) - 1)


def row_iota(shape):
    return lax.broadcasted_iota(jnp.int32, shape, len(shape) - 2)


def lane_swap(x, step):
    odd = (lane_iota(x.shape) & step) != 0
    return jnp.where(odd, pltpu.roll(x, step, 1), pltpu.roll(x, 128 - step, 1))


def lane_xor(x, amount, bits):
    for bit in bits:
        flip = ((amount >> bit) & 1) != 0
        x = jnp.where(flip, lane_swap(x, 1 << bit), x)
    return x


def place():
    gx, gy, gz = (lax.axis_index(name) for name in AXES)
    chip = (gx >> 1) * 64 + (gz & 1) * 32 + (gx & 1) * 16 + (gy >> 1) * 8 + (gz >> 1)
    return chip, gy & 1, gx * 4 + gy


def fill_rows(right_ref, dil_ref, rows_ref):
    dilution = jnp.broadcast_to(jnp.concatenate([dil_ref[...], dil_ref[...]], axis=1), (128, 128))
    spin_of = jnp.transpose(dilution)[0:64, :]
    pick = []
    for spin in range(4):
        one = jnp.where(spin_of == spin, 1.0, 0.0).astype(jnp.bfloat16)
        pick.append(jnp.concatenate([one] * 4, axis=1))
    for part in range(2):
        for colour in range(3):
            at = (part * 3 + colour) * 512
            noise = None
            for spin in range(4):
                rows_ref[spin * 64 : spin * 64 + 64, at : at + 512] = right_ref[spin, part, colour, 0:64, :]
                term = right_ref[spin, part, colour, 64:128, :] * pick[spin]
                noise = term if noise is None else noise + term
            rows_ref[256:320, at : at + 512] = noise


def add_tile(step, left_ref, rows_ref, out_ref):
    cols = []
    for part in range(2):
        for colour in range(3):
            pieces = []
            for tile in range(2):
                lines = slice(step * 32 + tile * 16, step * 32 + tile * 16 + 16)
                for spin in range(4):
                    pieces.append(left_ref[spin, part, colour, lines, :])
                for spin in range(4):
                    other = left_ref[spin, 1 - part, colour, lines, :]
                    pieces.append(-other if part == 0 else other)
            cols.append(jnp.concatenate(pieces, axis=0))
    prod = lax.dot_general(
        rows_ref[...],
        jnp.concatenate(cols, axis=1),
        (((1,), (1,)), ((), ())),
        preferred_element_type=jnp.float32,
    )
    low_i = lane_iota((8, 128)) & 15
    within = row_iota((8, 128)) ^ (low_i & 7)
    upper = low_i >= 8
    for tile in range(2):
        i_high = step * 2 + tile
        for block in range(20):
            first = prod[block * 16 : block * 16 + 8, tile * 128 : tile * 128 + 128]
            second = prod[block * 16 + 8 : block * 16 + 16, tile * 128 : tile * 128 + 128]
            j_high = block % 4 if block < 16 else block - 12
            start = (i_high ^ j_high) * (16 * ROWS) + block
            low_half = jnp.take_along_axis(jnp.where(upper, second, first), within, axis=0)
            high_half = jnp.take_along_axis(jnp.where(upper, first, second), within, axis=0)
            out_ref[pl.ds(start, 8, stride=ROWS), :] = low_half
            out_ref[pl.ds(start + 8 * ROWS, 8, stride=ROWS), :] = high_half


def away_kernel(left_ref, right_ref, dil_ref, out_ref, next_left_ref, next_right_ref, rows_ref, left_buf, right_buf, sems):
    _, core, _ = place()
    right_copies = [
        pltpu.make_async_copy(right_ref.at[1 - core, spin], right_buf.at[spin], sems.at[spin]) for spin in range(4)
    ]
    left_copies = []
    for step in range(4):
        lines = pl.ds(step * 32, 32)
        left_copies.append(
            pltpu.make_async_copy(
                left_ref.at[1 - core, :, :, :, lines, :], left_buf.at[:, :, :, lines, :], sems.at[4 + step]
            )
        )
    next_copies = [
        pltpu.make_async_copy(right_ref.at[core], next_right_ref, sems.at[8]),
        pltpu.make_async_copy(left_ref.at[core], next_left_ref, sems.at[9]),
    ]
    for copy in right_copies + left_copies:
        copy.start()
    for copy in right_copies:
        copy.wait()
    for copy in next_copies:
        copy.start()
    fill_rows(right_buf, dil_ref, rows_ref)
    for step in range(4):
        left_copies[step].wait()
        add_tile(step, left_buf, rows_ref, out_ref)
    for copy in next_copies:
        copy.wait()


def home_kernel(left_ref, right_ref, dil_ref, out_ref, rows_ref):
    fill_rows(right_ref, dil_ref, rows_ref)
    for step in range(4):
        add_tile(step, left_ref, rows_ref, out_ref)


def products(left, right, dil):
    slot = (4, 2, 3, 128, 512)
    rows = pltpu.VMEM((320, 3072), jnp.bfloat16)
    whole = pltpu.VMEM((CHIPS * ROWS, 128), jnp.float32)
    away, next_left, next_right = pl.pallas_call(
        away_kernel,
        in_specs=[HBM_SPEC, HBM_SPEC, VMEM_SPEC],
        out_specs=[VMEM_SPEC] * 3,
        out_shape=[whole, pltpu.VMEM(slot, jnp.bfloat16), pltpu.VMEM(slot, jnp.bfloat16)],
        scratch_shapes=[
            rows,
            pltpu.VMEM(slot, jnp.bfloat16),
            pltpu.VMEM(slot, jnp.bfloat16),
            pltpu.SemaphoreType.DMA((10,)),
        ],
        compiler_params=pltpu.CompilerParams(vmem_limit_bytes=16 << 20),
        name="away",
    )(*(pltpu.with_memory_space_constraint(x, pltpu.MemorySpace.HBM) for x in (left, right)), dil)
    arrived = lax.ppermute(away, AXES, PARTNER)
    home = pl.pallas_call(
        home_kernel,
        in_specs=[VMEM_SPEC] * 3,
        out_specs=VMEM_SPEC,
        out_shape=whole,
        scratch_shapes=[rows],
        compiler_params=pltpu.CompilerParams(vmem_limit_bytes=12 << 20),
        name="home",
    )(in_vmem(next_left), in_vmem(next_right), dil)
    return call(add_kernel, "add", whole, in_vmem(home), in_vmem(arrived))


def add_kernel(a_ref, b_ref, out_ref):
    out_ref[...] = a_ref[...] + b_ref[...]


def sum_planes_kernel(parts_ref, out_ref):
    total = parts_ref[0:160, :]
    for k in range(1, 16):
        total = total + parts_ref[k * 160 : k * 160 + 160, :]
    for z in range(8):
        mine = total[z * ROWS : z * ROWS + ROWS]
        out_ref[z * 40 : z * 40 + 40, :] = jnp.concatenate([mine, mine], axis=0)


def dot_exact(a, b, dims):
    return lax.dot_general(a, b, (dims, ((), ())), precision=EXACT, preferred_element_type=jnp.float32)


def combine_kernel(parts_ref, cols_ref, phase_ref, dil_ref, out_ref):
    chip, core, _ = place()
    coef = coefficients(cols_ref[...], phase_ref[...])
    lane8 = lane_iota((8, 128))
    row8 = row_iota((8, 128))
    dilution = jnp.broadcast_to(jnp.concatenate([dil_ref[...], dil_ref[...]], axis=1), (8, 128))
    spin_of = lane_xor(dilution, chip & 15, range(4))
    noise_lane = lane8 >= 64
    fields = []
    total = parts_ref[0:40, :]
    for z in range(1, 8):
        total = total + parts_ref[z * 40 : z * 40 + 40, :]
    for time in range(2):
        own = total[time * ROWS : time * ROWS + ROWS]
        terms = []
        for spin in range(4):
            x = jnp.concatenate([own[spin * 4 : spin * 4 + 4], own[16:20]], axis=0)
            for level in range(3):
                row_bit = (row8 >> level) & 1
                lane_bit = (lane8 >> (level + 4)) & 1
                up = pltpu.roll(pltpu.roll(x, 1 << level, 0), 128 - (16 << level), 1)
                down = pltpu.roll(pltpu.roll(x, 8 - (1 << level), 0), 16 << level, 1)
                x = jnp.where(row_bit == lane_bit, x, jnp.where(row_bit == 1, up, down))
            keep = jnp.logical_or(jnp.logical_not(noise_lane), spin_of == spin)
            terms.append(jnp.where(keep, x, 0.0))
        fields.append(dot_exact(coef, jnp.concatenate(terms, axis=0), ((0,), (0,))))
    both = jnp.concatenate(fields, axis=0)
    mirror = lane_xor(both, chip, range(7))
    cross = dot_exact(both, mirror, ((1,), (1,)))
    columns = []
    for time in range(2):
        real = cross[time * 32 : time * 32 + 16]
        imag = cross[time * 32 + 16 : time * 32 + 32]
        for at in (0, 32):
            columns.append(real[:, at : at + 16] - imag[:, at + 16 : at + 32])
            columns.append(real[:, at + 16 : at + 32] + imag[:, at : at + 16])
    trace_rows = jnp.concatenate(columns, axis=1)
    ordered = lane_xor(both, chip & 112, range(4, 7))
    ordered = jnp.where(core == 0, ordered, pltpu.roll(ordered, 120, 1))
    lane = lane_iota((16, 128))
    for pair in range(8):
        rows = jnp.zeros((16, 128), jnp.float32)
        for k in range(4):
            moved = pltpu.roll(ordered[k * 16 : k * 16 + 16], (8 * k - 16 * pair) % 128, 1)
            rows = jnp.where((lane >> 3) == k, moved, rows)
        out_ref[pl.ds(pair * 32, 16, stride=2), :] = trace_rows
        out_ref[pl.ds(pair * 32 + 1, 16, stride=2), :] = rows


def finish_kernel(pairs_ref, got_ref, fields_ref, traces_ref):
    _, _, block = place()
    row = row_iota((32, 128))
    pieces = []
    total = None
    for high in range(16):
        x_high, y_high, x_low, y_low = ((high >> k) & 1 for k in (3, 2, 1, 0))
        at = (x_high * 4 + x_low * 2 + y_low) * 32 + y_high * 2
        piece = got_ref[pl.ds(at, 8, stride=4), :]
        total = piece if total is None else total + piece
        pieces.append(got_ref[pl.ds(at + 1, 8, stride=4), :])
    sums = jnp.sum(total, axis=0, keepdims=True)
    x = jnp.transpose(jnp.concatenate(pieces, axis=0))[0:32, :]
    x = lane_xor(x, block * 8, range(3, 7))
    for bit in range(3):
        x = jnp.where(((row >> bit) & 1) != 0, lane_swap(x, 1 << bit), x)
    for time in range(2):
        for part in range(2):
            at = (time * 2 + part) * 8
            fields_ref[0, time, part] = x[at : at + 8]
    for pair in range(4):
        first = jnp.where(pairs_ref[0, pair] == 0, sums[:, 0:64], sums[:, 64:128])
        picked = jnp.where(pairs_ref[1, pair] == 0, first[:, 0:32], first[:, 32:64]) / 128.0
        traces_ref[pair, 0, 0:1, :] = picked[:, 0:16]
        traces_ref[pair, 0, 1:2, :] = picked[:, 16:32]


def coefficients(cols, phase):
    real = jnp.where(phase == 0, 1.0, jnp.where(phase == 2, -1.0, 0.0))
    imag = jnp.where(phase == 1, 1.0, jnp.where(phase == 3, -1.0, 0.0))
    blocks = []
    for spin in range(4):
        here = jnp.where(cols == spin, 1.0, 0.0)
        blocks.append(jnp.concatenate([here * real, here * imag], axis=1))
        blocks.append(jnp.concatenate([-here * imag, here * real], axis=1))
    return jnp.concatenate(blocks, axis=0)


def in_vmem(x):
    return pltpu.with_memory_space_constraint(x, VMEM)


VMEM_SPEC = pl.BlockSpec(memory_space=VMEM)
HBM_SPEC = pl.BlockSpec(memory_space=pltpu.MemorySpace.HBM)
SMEM_SPEC = pl.BlockSpec(memory_space=pltpu.MemorySpace.SMEM)


def call(kernel, name, out_shape, *operands, specs=None):
    return pl.pallas_call(
        kernel,
        in_specs=specs or [VMEM_SPEC] * len(operands),
        out_specs=jax.tree.map(lambda _: VMEM_SPEC, out_shape),
        out_shape=out_shape,
        compiler_params=pltpu.CompilerParams(vmem_limit_bytes=8 << 20),
        name=name,
    )(*operands)


def local(left_modes, right_modes, gamma_cols, gamma_phase, dilution, time_pairs):
    left = jnp.transpose(left_modes, (0, 1, 2, 4, 3, 5))
    right = jnp.transpose(right_modes, (0, 1, 2, 4, 3, 5))
    dil = dilution.reshape(1, 64)

    partial = products(left, right, dil).reshape(16, 160, 128)
    parts = lax.all_to_all(partial, AXES, 0, 0, axis_index_groups=PLANES, tiled=True)
    plane = call(sum_planes_kernel, "sum_planes", pltpu.VMEM((320, 128), jnp.float32), in_vmem(parts.reshape(2560, 128)))
    parts = lax.all_to_all(plane.reshape(16, 1, 2560), AXES, 0, 0, axis_index_groups=COLUMNS, tiled=True)
    rows = call(
        combine_kernel,
        "combine",
        pltpu.VMEM((256, 128), jnp.float32),
        in_vmem(parts.reshape(320, 128)),
        in_vmem(gamma_cols.T),
        in_vmem(gamma_phase.T),
        in_vmem(dil),
    )
    got = lax.all_to_all(rows.reshape(128, 2, 128), AXES, 0, 0, axis_index_groups=SAME_CORE, tiled=True)
    fields, traces = pl.pallas_call(
        finish_kernel,
        in_specs=[SMEM_SPEC, VMEM_SPEC],
        out_specs=[VMEM_SPEC, VMEM_SPEC],
        out_shape=[
            jax.ShapeDtypeStruct((1, 2, 2, 8, 128), jnp.float32),
            jax.ShapeDtypeStruct((4, 1, 2, 16), jnp.float32),
        ],
        name="finish",
    )(time_pairs.T, in_vmem(got.reshape(256, 128)))
    return (fields, jnp.swapaxes(traces, 2, 3))


def solution(mesh):
    return jax.shard_map(
        local,
        mesh=mesh,
        in_specs=(
            P(None, None, None, None, None, AXES),
            P(None, None, None, None, None, AXES),
            P(),
            P(),
            P(),
            P(),
        ),
        out_specs=(P("gz", None, None, ("gx", "gy"), None), P(None, "gz", None, None)),
        check_vma=False,
    )
```

time: 83.4 us -> 78.4 us (0.940)
  blocking collectives: 39.7 us -> 60.3 us
  waiting for transfers between devices: 13.2 us -> 0.4 us
  starting transfers between devices: 11.7 us -> 3.29 us
  Pallas kernels: 15.7 us -> 12.8 us
  other arithmetic: 1.45 us -> 0 us
    all_to_all x1 -> x2, blocking collectives: 15.5 us -> 36.1 us  [the longest x1 19.2 us: local(): lax.all_to_all(plane.reshape(16, 1, 2560), AXES, 0, 0, axis_index_groups=...]
    all_to_all x1 -> x0, waiting for transfers between devices: 12.4 us -> none  [local(): got = lax.all_to_all(rows.reshape(256, 1, 128), AXES, 0, 0, tiled=True)]
    all_to_all x1 -> x0, starting transfers between devices: 5.36 us -> none  [local(): got = lax.all_to_all(rows.reshape(256, 1, 128), AXES, 0, 0, tiled=True)]
    ppermute x2 -> x1, starting transfers between devices: 6.33 us -> 3.29 us  [products(): arrived = lax.ppermute(away, AXES, PARTNER)]
    pallas_call x2, Pallas kernels: 11.7 us -> 9.3 us  [the longest x1 7.05 us: products(): pl.pallas_call(away_kernel, in_specs=[HBM_SPEC, HBM_SPEC, VMEM_SPEC], out...]
    add x1 -> x0, other arithmetic: 1.45 us -> none  [local(): partial = (home + arrived).reshape(16, 160, 128)]
  transfers between devices with their start and end apart: 3 -> 1, of which waited for: 2 -> 1; matrix products, arithmetic and copies ran while one was open for 1% -> 0% of each run, Pallas kernels for 7% -> 3%
where the time goes in v3:
time: 78.4 us; the launch traced here: 78.2 us
  blocking collectives  60.3 us (77%)
  Pallas kernels  12.8 us (16%)
  starting transfers between devices  3.29 us (4%)
    all_to_all x1, blocking collectives, local(): lax.all_to_all(partial, AXES, 0, 0, axis_index_groups=PLANES, tiled=True)  24.3 us
    all_to_all x1, blocking collectives, local(): lax.all_to_all(plane.reshape(16, 1, 2560), AXES, 0, 0, axis_index_groups=...  19.2 us
    all_to_all x1, blocking collectives, local(): lax.all_to_all(rows.reshape(128, 2, 128), AXES, 0, 0, axis_index_groups=S...  16.8 us
    pallas_call x1, Pallas kernels, products(): pl.pallas_call(away_kernel, in_specs=[HBM_SPEC, HBM_SPEC, VMEM_SPEC], out...  7.05 us
    ppermute x1, starting transfers between devices, products(): arrived = lax.ppermute(away, AXES, PARTNER)  3.29 us
    pallas_call x1, Pallas kernels, products(): pl.pallas_call(home_kernel, in_specs=[VMEM_SPEC] * 3, out_specs=VMEM_SPEC...  2.25 us
    pallas_call x1, Pallas kernels, local(): pl.pallas_call(finish_kernel, in_specs=[SMEM_SPEC, VMEM_SPEC], out_specs=...  1.87 us
    pallas_call x3, Pallas kernels, call(): pl.pallas_call(kernel, in_specs=specs or [VMEM_SPEC] * len(operands), out...  1.67 us
  transfers between devices with their start and end apart: 1, of which 1 were waited for; matrix products, arithmetic and copies ran while one was open for 0% of the time, Pallas kernels for 3%

profile of v3, /device:TPU:1, one launch (start us, length us, event | category | flops | bytes accessed | tf_op | source)
XLA Modules:
  0.0 78.2 jit_solution(2043152234473610115)
XLA Ops:
  0.6 0.0 copy-start
  0.6 0.6 copy-done
  1.3 7.1 %away.1 = (f32[2560,128]{1,0:T(8,128)S(1)}, bf16[4,2,3,128,512]{4,3,2,1,0:T(8,128)(2,1)S(1)}, bf16[4,2,3,128,512]{4,3,2,1,0:T(8,128)(2,1)S(1)}) custom-call(bf16[2,4,2,3,128,512]{5,4,3,2,1,0:T(8,128)(2,1)} %bitcast.24, bf16[2,4,2,3,128,512]{5,4,3,2,1,0:T(8,128)(2,1)} %bitcast.25, s32[1,64]{1,0:T(1,128)S(1)} %bitcast.19), custom_call_target="tpu_custom_call" | custom-call | tf_op jit(solution)/shard_map/away/pallas_call | solution.py:146
  8.3 3.3 %collective-permute-start = (f32[2560,128]{1,0:T(8,128)S(1)}, f32[2560,128]{1,0:T(8,128)S(1)}, u32[]{:S(2)}, u32[]{:S(2)}) collective-permute-start(f32[2560,128]{1,0:T(8,128)S(1)} %get-tuple-element.9), channel_id=1, source_target_pairs={{0,16},{16,0},{2,18},{18,2},{4,20},{20,4},{6,22},{22,6},{8,24},{24... | collective-permute-start | bytes 3932168 | tf_op jit(solution)/shard_map/ppermute | solution.py:160
  11.6 2.2 %home.1.a_ref = f32[2560,128]{1,0:T(8,128)S(1)} custom-call(bf16[4,2,3,128,512]{4,3,2,1,0:T(8,128)(2,1)S(1)} %get-tuple-element.7.left_ref, bf16[4,2,3,128,512]{4,3,2,1,0:T(8,128)(2,1)S(1)} %get-tuple-element.8.right_ref, s32[1,64]{1,0:T(1,128)S(1)} %bitcast.20), custom_call_target="tpu_custom_call" | custom-call | tf_op jit(solution)/shard_map/home/pallas_call | solution.py:161
  13.9 0.4 collective-permute-done.b_ref
  14.3 0.1 add.1
  14.4 24.3 %all_to_all.15 = f32[16,160,128]{2,1,0:T(8,128)S(1)} all-to-all(f32[16,160,128]{2,1,0:T(8,128)S(1)} %bitcast.14), channel_id=1, replica_groups={{0,32,64,96,1,33,65,97,128,160,192,224,129,161,193,225},{16,48,80,112,1..., dimensions={0} | all-to-all | bytes 2621440 | tf_op jit(solution)/shard_map/all_to_all | solution.py:303
  38.7 0.0 copy-start.1
  38.7 0.0 copy-start.2
  38.7 0.1 sum_planes.1
  38.8 19.2 %all_to_all.16 = f32[16,1,2560]{2,1,0:T(1,128)S(1)} all-to-all(f32[16,1,2560]{2,1,0:T(1,128)S(1)} %bitcast.16), channel_id=1, replica_groups={{0,16,2,18,4,20,6,22,8,24,10,26,12,28,14,30},{32,48,34,50,36,52,38,54,4..., dimensions={0} | all-to-all | bytes 327680 | tf_op jit(solution)/shard_map/all_to_all | solution.py:305
  58.0 0.0 copy-done.1
  58.0 0.0 copy-done.2
  58.0 1.5 %combine.1 = f32[256,128]{1,0:T(8,128)S(1)} custom-call(f32[320,128]{1,0:T(8,128)S(1)} %bitcast.15, s32[4,16]{1,0:T(4,128)S(1)} %bitcast.22, s32[4,16]{1,0:T(4,128)S(1)} %bitcast.23, s32[1,64]{1,0:T(1,128)S(1)} %bitcast.21), custom_call_target="tpu_custom_call" | custom-call | tf_op jit(solution)/shard_map/combine/pallas_call | solution.py:287
  59.5 16.8 %all_to_all.17 = f32[128,2,128]{2,1,0:T(2,128)S(1)} all-to-all(f32[128,2,128]{2,1,0:T(2,128)S(1)} %bitcast.17), channel_id=1, replica_groups={{0,1,2,3,4,5,6,7,8,9,10,11,12,13,14,15,32,33,34,35,36,37,38,39,40,41,42..., dimensions={0} | all-to-all | bytes 262144 | tf_op jit(solution)/shard_map/all_to_all | solution.py:315
  76.3 1.9 %finish.1 = (f32[1,2,2,8,128]{4,3,2,1,0:T(8,128)}, f32[4,1,2,16]{3,2,1,0:T(2,128)}) custom-call(s32[2,4]{1,0:T(2,128)} %bitcast.26, f32[256,128]{1,0:T(8,128)S(1)} %bitcast.18), custom_call_target="tpu_custom_call" | custom-call | tf_op jit(solution)/shard_map/finish/pallas_call | solution.py:316
Async XLA Ops:
  0.6 0.7 copy-start
  8.3 5.9 %collective-permute-start = (f32[2560,128]{1,0:T(8,128)S(1)}, f32[2560,128]{1,0:T(8,128)S(1)}, u32[]{:S(2)}, u32[]{:S(2)}) collective-permute-start(f32[2560,128]{1,0:T(8,128)S(1)} %get-tuple-element.9), channel_id=1, source_target_pairs={{0,16},{16,0},{2,18},{18,2},{4,20},{20,4},{6,22},{22,6},{8,24},{24... | collective-permute-start | bytes 3932168 | tf_op jit(solution)/shard_map/ppermute | solution.py:160
  38.7 19.3 %copy-start.1 = (s32[16,4]{0,1:T(4,128)S(1)}, s32[16,4]{0,1:T(4,128)}, u32[]{:S(2)}) copy-start(s32[16,4]{0,1:T(4,128)} %param.8) | copy-start | bytes 772
  38.7 19.3 %copy-start.2 = (s32[16,4]{0,1:T(4,128)S(1)}, s32[16,4]{0,1:T(4,128)}, u32[]{:S(2)}) copy-start(s32[16,4]{0,1:T(4,128)} %param.9) | copy-start | bytes 772

commit v4 on v3

--- a/solution.py
+++ b/solution.py
@@ -102,32 +102,34 @@
             out_ref[pl.ds(start + 8 * ROWS, 8, stride=ROWS), :] = high_half
 
 
-def away_kernel(left_ref, right_ref, dil_ref, out_ref, next_left_ref, next_right_ref, rows_ref, left_buf, right_buf, sems):
+def away_kernel(
+    left_ref, right_ref, dil_ref, out_ref, next_left_ref, next_right_ref, next_dil_ref, rows_ref, left_buf, right_buf, sems
+):
     _, core, _ = place()
-    right_copies = [
-        pltpu.make_async_copy(right_ref.at[1 - core, spin], right_buf.at[spin], sems.at[spin]) for spin in range(4)
-    ]
-    left_copies = []
+    copies = [pltpu.make_async_copy(dil_ref, next_dil_ref, sems.at[0])]
+    for spin in range(4):
+        for part in range(2):
+            at = (spin, part)
+            sem = sems.at[1 + spin * 2 + part]
+            copies.append(pltpu.make_async_copy(right_ref.at[(1 - core,) + at], right_buf.at[at], sem))
+    for spin in range(4):
+        for part in range(2):
+            at = (spin, part)
+            sem = sems.at[9 + spin * 2 + part]
+            copies.append(pltpu.make_async_copy(left_ref.at[(1 - core,) + at], left_buf.at[at], sem))
+    next_copies = []
+    for which, (source, target) in enumerate(((right_ref, next_right_ref), (left_ref, next_left_ref))):
+        for spin in range(4):
+            for part in range(2):
+                at = (spin, part)
+                sem = sems.at[17 + which * 8 + spin * 2 + part]
+                next_copies.append(pltpu.make_async_copy(source.at[(core,) + at], target.at[at], sem))
+    for copy in copies + next_copies:
+        copy.start()
+    for copy in copies:
+        copy.wait()
+    fill_rows(right_buf, next_dil_ref, rows_ref)
     for step in range(4):
-        lines = pl.ds(step * 32, 32)
-        left_copies.append(
-            pltpu.make_async_copy(
-                left_ref.at[1 - core, :, :, :, lines, :], left_buf.at[:, :, :, lines, :], sems.at[4 + step]
-            )
-        )
-    next_copies = [
-        pltpu.make_async_copy(right_ref.at[core], next_right_ref, sems.at[8]),
-        pltpu.make_async_copy(left_ref.at[core], next_left_ref, sems.at[9]),
-    ]
-    for copy in right_copies + left_copies:
-        copy.start()
-    for copy in right_copies:
-        copy.wait()
-    for copy in next_copies:
-        copy.start()
-    fill_rows(right_buf, dil_ref, rows_ref)
-    for step in range(4):
-        left_copies[step].wait()
         add_tile(step, left_buf, rows_ref, out_ref)
     for copy in next_copies:
         copy.wait()
@@ -143,20 +145,20 @@
     slot = (4, 2, 3, 128, 512)
     rows = pltpu.VMEM((320, 3072), jnp.bfloat16)
     whole = pltpu.VMEM((CHIPS * ROWS, 128), jnp.float32)
-    away, next_left, next_right = pl.pallas_call(
+    away, next_left, next_right, next_dil = pl.pallas_call(
         away_kernel,
-        in_specs=[HBM_SPEC, HBM_SPEC, VMEM_SPEC],
-        out_specs=[VMEM_SPEC] * 3,
-        out_shape=[whole, pltpu.VMEM(slot, jnp.bfloat16), pltpu.VMEM(slot, jnp.bfloat16)],
+        in_specs=[HBM_SPEC] * 3,
+        out_specs=[VMEM_SPEC] * 4,
+        out_shape=[whole, pltpu.VMEM(slot, jnp.bfloat16), pltpu.VMEM(slot, jnp.bfloat16), pltpu.VMEM((1, 64), jnp.int32)],
         scratch_shapes=[
             rows,
             pltpu.VMEM(slot, jnp.bfloat16),
             pltpu.VMEM(slot, jnp.bfloat16),
-            pltpu.SemaphoreType.DMA((10,)),
+            pltpu.SemaphoreType.DMA((33,)),
         ],
         compiler_params=pltpu.CompilerParams(vmem_limit_bytes=16 << 20),
         name="away",
-    )(*(pltpu.with_memory_space_constraint(x, pltpu.MemorySpace.HBM) for x in (left, right)), dil)
+    )(*(pltpu.with_memory_space_constraint(x, pltpu.MemorySpace.HBM) for x in (left, right, dil)))
     arrived = lax.ppermute(away, AXES, PARTNER)
     home = pl.pallas_call(
         home_kernel,
@@ -166,8 +168,8 @@
         scratch_shapes=[rows],
         compiler_params=pltpu.CompilerParams(vmem_limit_bytes=12 << 20),
         name="home",
-    )(in_vmem(next_left), in_vmem(next_right), dil)
-    return call(add_kernel, "add", whole, in_vmem(home), in_vmem(arrived))
+    )(in_vmem(next_left), in_vmem(next_right), in_vmem(next_dil))
+    return call(add_kernel, "add", whole, in_vmem(home), in_vmem(arrived)), next_dil
 
 
 def add_kernel(a_ref, b_ref, out_ref):
@@ -299,7 +301,8 @@
     right = jnp.transpose(right_modes, (0, 1, 2, 4, 3, 5))
     dil = dilution.reshape(1, 64)
 
-    partial = products(left, right, dil).reshape(16, 160, 128)
+    partial, dil = products(left, right, dil)
+    partial = partial.reshape(16, 160, 128)
     parts = lax.all_to_all(partial, AXES, 0, 0, axis_index_groups=PLANES, tiled=True)
     plane = call(sum_planes_kernel, "sum_planes", pltpu.VMEM((320, 128), jnp.float32), in_vmem(parts.reshape(2560, 128)))
     parts = lax.all_to_all(plane.reshape(16, 1, 2560), AXES, 0, 0, axis_index_groups=COLUMNS, tiled=True)

time: 78.4 us -> 76.1 us (0.971)
  Pallas kernels: 12.8 us -> 11.1 us
    pallas_call x1, Pallas kernels: 7.05 us -> 5.35 us  [products(): pl.pallas_call(away_kernel, in_specs=[HBM_SPEC] * 3, out_specs=[VMEM_SPEC...]
where the time goes in v4:
time: 76.1 us; the launch traced here: 75.8 us
  blocking collectives  60.4 us (79%)
  Pallas kernels  11.1 us (15%)
  starting transfers between devices  3.29 us (4%)
    all_to_all x1, blocking collectives, local(): lax.all_to_all(partial, AXES, 0, 0, axis_index_groups=PLANES, tiled=True)  24.3 us
    all_to_all x1, blocking collectives, local(): lax.all_to_all(plane.reshape(16, 1, 2560), AXES, 0, 0, axis_index_groups=...  19.2 us
    all_to_all x1, blocking collectives, local(): lax.all_to_all(rows.reshape(128, 2, 128), AXES, 0, 0, axis_index_groups=S...  16.8 us
    pallas_call x1, Pallas kernels, products(): pl.pallas_call(away_kernel, in_specs=[HBM_SPEC] * 3, out_specs=[VMEM_SPEC...  5.35 us
    ppermute x1, starting transfers between devices, products(): arrived = lax.ppermute(away, AXES, PARTNER)  3.29 us
    pallas_call x1, Pallas kernels, products(): pl.pallas_call(home_kernel, in_specs=[VMEM_SPEC] * 3, out_specs=VMEM_SPEC...  2.25 us
    pallas_call x1, Pallas kernels, local(): pl.pallas_call(finish_kernel, in_specs=[SMEM_SPEC, VMEM_SPEC], out_specs=...  1.87 us
    pallas_call x3, Pallas kernels, call(): pl.pallas_call(kernel, in_specs=specs or [VMEM_SPEC] * len(operands), out...  1.67 us
  transfers between devices with their start and end apart: 1, of which 1 were waited for; matrix products, arithmetic and copies ran while one was open for 0% of the time, Pallas kernels for 3%

profile of v4, /device:TPU:1, one launch (start us, length us, event | category | flops | bytes accessed | tf_op | source)
XLA Modules:
  0.0 75.8 jit_solution(8462511238513704063)
XLA Ops:
  0.6 5.3 %away.1 = (f32[2560,128]{1,0:T(8,128)S(1)}, bf16[4,2,3,128,512]{4,3,2,1,0:T(8,128)(2,1)S(1)}, bf16[4,2,3,128,512]{4,3,2,1,0:T(8,128)(2,1)S(1)}, s32[1,64]{1,0:T(1,128)S(1)}) custom-call(bf16[2,4,2,3,128,512]{5,4,3,2,1,0:T(8,128)(2,1)} %bitcast.21, bf16[2,4,2,3,128,512]{5,4,3,2,1,0:T(8,128)(2,1)} %bitcast.22, s32[1,64]{1,0:T(1,128)} %bitcast.24), custom_call_target="tpu_custom_call" | custom-call | tf_op jit(solution)/shard_map/away/pallas_call | solution.py:148
  6.0 3.3 %collective-permute-start = (f32[2560,128]{1,0:T(8,128)S(1)}, f32[2560,128]{1,0:T(8,128)S(1)}, u32[]{:S(2)}, u32[]{:S(2)}) collective-permute-start(f32[2560,128]{1,0:T(8,128)S(1)} %get-tuple-element.11), channel_id=1, source_target_pairs={{0,16},{16,0},{2,18},{18,2},{4,20},{20,4},{6,22},{22,6},{8,24},{24... | collective-permute-start | bytes 3932168 | tf_op jit(solution)/shard_map/ppermute | solution.py:162
  9.3 2.2 %home.1.a_ref = f32[2560,128]{1,0:T(8,128)S(1)} custom-call(bf16[4,2,3,128,512]{4,3,2,1,0:T(8,128)(2,1)S(1)} %get-tuple-element.8.left_ref, bf16[4,2,3,128,512]{4,3,2,1,0:T(8,128)(2,1)S(1)} %get-tuple-element.9.right_ref, s32[1,64]{1,0:T(1,128)S(1)} %get-tuple-element.10.dil_ref), custom_call_target="tpu_custom_call" | custom-call | tf_op jit(solution)/shard_map/home/pallas_call | solution.py:163
  11.5 0.4 collective-permute-done.b_ref
  11.9 0.1 add.1
  12.1 24.3 %all_to_all.15 = f32[16,160,128]{2,1,0:T(8,128)S(1)} all-to-all(f32[16,160,128]{2,1,0:T(8,128)S(1)} %bitcast.14), channel_id=1, replica_groups={{0,32,64,96,1,33,65,97,128,160,192,224,129,161,193,225},{16,48,80,112,1..., dimensions={0} | all-to-all | bytes 2621440 | tf_op jit(solution)/shard_map/all_to_all | solution.py:306
  36.4 0.0 copy-start
  36.4 0.0 copy-start.1
  36.4 0.1 sum_planes.1
  36.4 19.2 %all_to_all.16 = f32[16,1,2560]{2,1,0:T(1,128)S(1)} all-to-all(f32[16,1,2560]{2,1,0:T(1,128)S(1)} %bitcast.16), channel_id=1, replica_groups={{0,16,2,18,4,20,6,22,8,24,10,26,12,28,14,30},{32,48,34,50,36,52,38,54,4..., dimensions={0} | all-to-all | bytes 327680 | tf_op jit(solution)/shard_map/all_to_all | solution.py:308
  55.7 0.0 copy-done
  55.7 0.0 copy-done.1
  55.7 1.5 %combine.1 = f32[256,128]{1,0:T(8,128)S(1)} custom-call(f32[320,128]{1,0:T(8,128)S(1)} %bitcast.15, s32[4,16]{1,0:T(4,128)S(1)} %bitcast.19, s32[4,16]{1,0:T(4,128)S(1)} %bitcast.20, s32[1,64]{1,0:T(1,128)S(1)} %get-tuple-element.10.dil_ref), custom_call_target="tpu_custom_call" | custom-call | tf_op jit(solution)/shard_map/combine/pallas_call | solution.py:289
  57.1 16.8 %all_to_all.17 = f32[128,2,128]{2,1,0:T(2,128)S(1)} all-to-all(f32[128,2,128]{2,1,0:T(2,128)S(1)} %bitcast.17), channel_id=1, replica_groups={{0,1,2,3,4,5,6,7,8,9,10,11,12,13,14,15,32,33,34,35,36,37,38,39,40,41,42..., dimensions={0} | all-to-all | bytes 262144 | tf_op jit(solution)/shard_map/all_to_all | solution.py:318
  74.0 1.9 %finish.1 = (f32[1,2,2,8,128]{4,3,2,1,0:T(8,128)}, f32[4,1,2,16]{3,2,1,0:T(2,128)}) custom-call(s32[2,4]{1,0:T(2,128)} %bitcast.23, f32[256,128]{1,0:T(8,128)S(1)} %bitcast.18), custom_call_target="tpu_custom_call" | custom-call | tf_op jit(solution)/shard_map/finish/pallas_call | solution.py:319
Async XLA Ops:
  6.0 6.0 %collective-permute-start = (f32[2560,128]{1,0:T(8,128)S(1)}, f32[2560,128]{1,0:T(8,128)S(1)}, u32[]{:S(2)}, u32[]{:S(2)}) collective-permute-start(f32[2560,128]{1,0:T(8,128)S(1)} %get-tuple-element.11), channel_id=1, source_target_pairs={{0,16},{16,0},{2,18},{18,2},{4,20},{20,4},{6,22},{22,6},{8,24},{24... | collective-permute-start | bytes 3932168 | tf_op jit(solution)/shard_map/ppermute | solution.py:162
  36.4 19.3 %copy-start = (s32[16,4]{0,1:T(4,128)S(1)}, s32[16,4]{0,1:T(4,128)}, u32[]{:S(2)}) copy-start(s32[16,4]{0,1:T(4,128)} %param.8) | copy-start | bytes 772
  36.4 19.3 %copy-start.1 = (s32[16,4]{0,1:T(4,128)S(1)}, s32[16,4]{0,1:T(4,128)}, u32[]{:S(2)}) copy-start(s32[16,4]{0,1:T(4,128)} %param.9) | copy-start | bytes 772

commit v5 on v4

--- a/solution.py
+++ b/solution.py
@@ -189,7 +189,7 @@
     return lax.dot_general(a, b, (dims, ((), ())), precision=EXACT, preferred_element_type=jnp.float32)
 
 
-def combine_kernel(parts_ref, cols_ref, phase_ref, dil_ref, out_ref):
+def combine_kernel(parts_ref, cols_ref, phase_ref, dil_ref, pairs_ref, out_ref):
     chip, core, _ = place()
     coef = coefficients(cols_ref[...], phase_ref[...])
     lane8 = lane_iota((8, 128))
@@ -218,13 +218,21 @@
     both = jnp.concatenate(fields, axis=0)
     mirror = lane_xor(both, chip, range(7))
     cross = dot_exact(both, mirror, ((1,), (1,)))
-    columns = []
+    crossed = []
     for time in range(2):
         real = cross[time * 32 : time * 32 + 16]
         imag = cross[time * 32 + 16 : time * 32 + 32]
         for at in (0, 32):
-            columns.append(real[:, at : at + 16] - imag[:, at + 16 : at + 32])
-            columns.append(real[:, at + 16 : at + 32] + imag[:, at : at + 16])
+            real_part = real[:, at : at + 16] - imag[:, at + 16 : at + 32]
+            imag_part = real[:, at + 16 : at + 32] + imag[:, at : at + 16]
+            crossed.append(jnp.concatenate([real_part, imag_part], axis=1))
+    columns = []
+    for pair in range(4):
+        first = jnp.broadcast_to(pairs_ref[0:1, pair : pair + 1], (16, 32)) == 0
+        second = jnp.broadcast_to(pairs_ref[1:2, pair : pair + 1], (16, 32)) == 0
+        columns.append(
+            jnp.where(first, jnp.where(second, crossed[0], crossed[1]), jnp.where(second, crossed[2], crossed[3]))
+        )
     trace_rows = jnp.concatenate(columns, axis=1)
     ordered = lane_xor(both, chip & 112, range(4, 7))
     ordered = jnp.where(core == 0, ordered, pltpu.roll(ordered, 120, 1))
@@ -238,7 +246,7 @@
         out_ref[pl.ds(pair * 32 + 1, 16, stride=2), :] = rows
 
 
-def finish_kernel(pairs_ref, got_ref, fields_ref, traces_ref):
+def finish_kernel(got_ref, fields_ref, traces_ref):
     _, _, block = place()
     row = row_iota((32, 128))
     pieces = []
@@ -258,11 +266,10 @@
         for part in range(2):
             at = (time * 2 + part) * 8
             fields_ref[0, time, part] = x[at : at + 8]
+    sums = sums / 128.0
     for pair in range(4):
-        first = jnp.where(pairs_ref[0, pair] == 0, sums[:, 0:64], sums[:, 64:128])
-        picked = jnp.where(pairs_ref[1, pair] == 0, first[:, 0:32], first[:, 32:64]) / 128.0
-        traces_ref[pair, 0, 0:1, :] = picked[:, 0:16]
-        traces_ref[pair, 0, 1:2, :] = picked[:, 16:32]
+        traces_ref[pair, 0, 0:1, :] = sums[:, pair * 32 : pair * 32 + 16]
+        traces_ref[pair, 0, 1:2, :] = sums[:, pair * 32 + 16 : pair * 32 + 32]
 
 
 def coefficients(cols, phase):
@@ -282,7 +289,6 @@
 
 VMEM_SPEC = pl.BlockSpec(memory_space=VMEM)
 HBM_SPEC = pl.BlockSpec(memory_space=pltpu.MemorySpace.HBM)
-SMEM_SPEC = pl.BlockSpec(memory_space=pltpu.MemorySpace.SMEM)
 
 
 def call(kernel, name, out_shape, *operands, specs=None):
@@ -314,18 +320,19 @@
         in_vmem(gamma_cols.T),
         in_vmem(gamma_phase.T),
         in_vmem(dil),
+        in_vmem(time_pairs.T),
     )
     got = lax.all_to_all(rows.reshape(128, 2, 128), AXES, 0, 0, axis_index_groups=SAME_CORE, tiled=True)
     fields, traces = pl.pallas_call(
         finish_kernel,
-        in_specs=[SMEM_SPEC, VMEM_SPEC],
+        in_specs=[VMEM_SPEC],
         out_specs=[VMEM_SPEC, VMEM_SPEC],
         out_shape=[
             jax.ShapeDtypeStruct((1, 2, 2, 8, 128), jnp.float32),
             jax.ShapeDtypeStruct((4, 1, 2, 16), jnp.float32),
         ],
         name="finish",
-    )(time_pairs.T, in_vmem(got.reshape(256, 128)))
+    )(in_vmem(got.reshape(256, 128)))
     return (fields, jnp.swapaxes(traces, 2, 3))
 
 

time: 76.1 us -> 75.4 us (level)
  no operation moved by 1% of the time
where the time goes in v5:
time: 75.4 us; the launch traced here: 75.2 us
  blocking collectives  60.4 us (80%)
  Pallas kernels  10.5 us (14%)
  starting transfers between devices  3.29 us (4%)
    all_to_all x1, blocking collectives, local(): lax.all_to_all(partial, AXES, 0, 0, axis_index_groups=PLANES, tiled=True)  24.3 us
    all_to_all x1, blocking collectives, local(): lax.all_to_all(plane.reshape(16, 1, 2560), AXES, 0, 0, axis_index_groups=...  19.2 us
    all_to_all x1, blocking collectives, local(): lax.all_to_all(rows.reshape(128, 2, 128), AXES, 0, 0, axis_index_groups=S...  16.8 us
    pallas_call x1, Pallas kernels, products(): pl.pallas_call(away_kernel, in_specs=[HBM_SPEC] * 3, out_specs=[VMEM_SPEC...  5.35 us
    ppermute x1, starting transfers between devices, products(): arrived = lax.ppermute(away, AXES, PARTNER)  3.29 us
    pallas_call x1, Pallas kernels, products(): pl.pallas_call(home_kernel, in_specs=[VMEM_SPEC] * 3, out_specs=VMEM_SPEC...  2.25 us
    pallas_call x3, Pallas kernels, call(): pl.pallas_call(kernel, in_specs=specs or [VMEM_SPEC] * len(operands), out...  1.71 us
  transfers between devices with their start and end apart: 1, of which 1 were waited for; matrix products, arithmetic and copies ran while one was open for 0% of the time, Pallas kernels for 3%

profile of v5, /device:TPU:1, one launch (start us, length us, event | category | flops | bytes accessed | tf_op | source)
XLA Modules:
  0.0 75.2 jit_solution(11329335377282335047)
XLA Ops:
  0.6 5.3 %away.1 = (f32[2560,128]{1,0:T(8,128)S(1)}, bf16[4,2,3,128,512]{4,3,2,1,0:T(8,128)(2,1)S(1)}, bf16[4,2,3,128,512]{4,3,2,1,0:T(8,128)(2,1)S(1)}, s32[1,64]{1,0:T(1,128)S(1)}) custom-call(bf16[2,4,2,3,128,512]{5,4,3,2,1,0:T(8,128)(2,1)} %bitcast.22, bf16[2,4,2,3,128,512]{5,4,3,2,1,0:T(8,128)(2,1)} %bitcast.23, s32[1,64]{1,0:T(1,128)} %bitcast.24), custom_call_target="tpu_custom_call" | custom-call | tf_op jit(solution)/shard_map/away/pallas_call | solution.py:148
  6.0 3.3 %collective-permute-start = (f32[2560,128]{1,0:T(8,128)S(1)}, f32[2560,128]{1,0:T(8,128)S(1)}, u32[]{:S(2)}, u32[]{:S(2)}) collective-permute-start(f32[2560,128]{1,0:T(8,128)S(1)} %get-tuple-element.11), channel_id=1, source_target_pairs={{0,16},{16,0},{2,18},{18,2},{4,20},{20,4},{6,22},{22,6},{8,24},{24... | collective-permute-start | bytes 3932168 | tf_op jit(solution)/shard_map/ppermute | solution.py:162
  9.3 2.2 %home.1.a_ref = f32[2560,128]{1,0:T(8,128)S(1)} custom-call(bf16[4,2,3,128,512]{4,3,2,1,0:T(8,128)(2,1)S(1)} %get-tuple-element.8.left_ref, bf16[4,2,3,128,512]{4,3,2,1,0:T(8,128)(2,1)S(1)} %get-tuple-element.9.right_ref, s32[1,64]{1,0:T(1,128)S(1)} %get-tuple-element.10.dil_ref), custom_call_target="tpu_custom_call" | custom-call | tf_op jit(solution)/shard_map/home/pallas_call | solution.py:163
  11.5 0.4 collective-permute-done.b_ref
  11.9 0.1 add.1
  12.1 24.3 %all_to_all.15 = f32[16,160,128]{2,1,0:T(8,128)S(1)} all-to-all(f32[16,160,128]{2,1,0:T(8,128)S(1)} %bitcast.14), channel_id=1, replica_groups={{0,32,64,96,1,33,65,97,128,160,192,224,129,161,193,225},{16,48,80,112,1..., dimensions={0} | all-to-all | bytes 2621440 | tf_op jit(solution)/shard_map/all_to_all | solution.py:312
  36.4 0.0 copy-start
  36.4 0.0 copy-start.1
  36.4 0.0 copy-start.2
  36.4 0.1 sum_planes.1
  36.4 19.2 %all_to_all.16 = f32[16,1,2560]{2,1,0:T(1,128)S(1)} all-to-all(f32[16,1,2560]{2,1,0:T(1,128)S(1)} %bitcast.16), channel_id=1, replica_groups={{0,16,2,18,4,20,6,22,8,24,10,26,12,28,14,30},{32,48,34,50,36,52,38,54,4..., dimensions={0} | all-to-all | bytes 327680 | tf_op jit(solution)/shard_map/all_to_all | solution.py:314
  55.7 0.0 copy-done
  55.7 0.0 copy-done.1
  55.7 0.0 copy-done.2
  55.7 1.5 %combine.1 = f32[256,128]{1,0:T(8,128)S(1)} custom-call(f32[320,128]{1,0:T(8,128)S(1)} %bitcast.15, s32[4,16]{1,0:T(4,128)S(1)} %bitcast.19, s32[4,16]{1,0:T(4,128)S(1)} %bitcast.20, s32[1,64]{1,0:T(1,128)S(1)} %get-tuple-element.10.dil_ref, s32[2,4]{1,0:T(2,128)S(1)} %bitcast.21), custom_call_target="tpu_custom_call" | custom-call | tf_op jit(solution)/shard_map/combine/pallas_call | solution.py:295
  57.2 16.8 %all_to_all.17 = f32[128,2,128]{2,1,0:T(2,128)S(1)} all-to-all(f32[128,2,128]{2,1,0:T(2,128)S(1)} %bitcast.17), channel_id=1, replica_groups={{0,1,2,3,4,5,6,7,8,9,10,11,12,13,14,15,32,33,34,35,36,37,38,39,40,41,42..., dimensions={0} | all-to-all | bytes 262144 | tf_op jit(solution)/shard_map/all_to_all | solution.py:325
  74.0 1.2 %finish.1 = (f32[1,2,2,8,128]{4,3,2,1,0:T(8,128)}, f32[4,1,2,16]{3,2,1,0:T(2,128)}) custom-call(f32[256,128]{1,0:T(8,128)S(1)} %bitcast.18), custom_call_target="tpu_custom_call" | custom-call | tf_op jit(solution)/shard_map/finish/pallas_call | solution.py:326
Async XLA Ops:
  6.0 6.0 %collective-permute-start = (f32[2560,128]{1,0:T(8,128)S(1)}, f32[2560,128]{1,0:T(8,128)S(1)}, u32[]{:S(2)}, u32[]{:S(2)}) collective-permute-start(f32[2560,128]{1,0:T(8,128)S(1)} %get-tuple-element.11), channel_id=1, source_target_pairs={{0,16},{16,0},{2,18},{18,2},{4,20},{20,4},{6,22},{22,6},{8,24},{24... | collective-permute-start | bytes 3932168 | tf_op jit(solution)/shard_map/ppermute | solution.py:162
  36.4 19.3 %copy-start = (s32[16,4]{0,1:T(4,128)S(1)}, s32[16,4]{0,1:T(4,128)}, u32[]{:S(2)}) copy-start(s32[16,4]{0,1:T(4,128)} %param.8) | copy-start | bytes 772
  36.4 19.3 %copy-start.1 = (s32[16,4]{0,1:T(4,128)S(1)}, s32[16,4]{0,1:T(4,128)}, u32[]{:S(2)}) copy-start(s32[16,4]{0,1:T(4,128)} %param.9) | copy-start | bytes 772
  36.4 19.3 %copy-start.2 = (s32[4,2]{0,1:T(2,128)S(1)}, s32[4,2]{0,1:T(2,128)}, u32[]{:S(2)}) copy-start(s32[4,2]{0,1:T(2,128)} %param.11) | copy-start | bytes 100

commit v6 on v5

--- a/solution.py
+++ b/solution.py
@@ -18,7 +18,7 @@
 
 
 PLANES = [[flat_index(plane * 8 + z, core) for plane in range(16)] for z in range(8) for core in range(2)]
-COLUMNS = [[flat_index(plane * 8 + z, core) for z in range(8) for core in range(2)] for plane in range(16)]
+COLUMNS = [[flat_index(plane * 8 + z, core) for core in range(2) for z in range(8)] for plane in range(16)]
 PARTNER = [(flat_index(chip, core), flat_index(chip, 1 - core)) for chip in range(CHIPS) for core in range(2)]
 SAME_CORE = [sorted(flat_index(chip, core) for chip in range(CHIPS)) for core in range(2)]
 
@@ -29,18 +29,6 @@
 
 def row_iota(shape):
     return lax.broadcasted_iota(jnp.int32, shape, len(shape) - 2)
-
-
-def lane_swap(x, step):
-    odd = (lane_iota(x.shape) & step) != 0
-    return jnp.where(odd, pltpu.roll(x, step, 1), pltpu.roll(x, 128 - step, 1))
-
-
-def lane_xor(x, amount, bits):
-    for bit in bits:
-        flip = ((amount >> bit) & 1) != 0
-        x = jnp.where(flip, lane_swap(x, 1 << bit), x)
-    return x
 
 
 def place():
@@ -103,10 +91,16 @@
 
 
 def away_kernel(
-    left_ref, right_ref, dil_ref, out_ref, next_left_ref, next_right_ref, next_dil_ref, rows_ref, left_buf, right_buf, sems
+    left_ref, right_ref, dil_ref, cols_ref, phase_ref, out_ref, next_left_ref, next_right_ref, next_dil_ref, coef_ref, spin_ref,
+    rows_ref, left_buf, right_buf, cols_buf, phase_buf, sems
 ):
-    _, core, _ = place()
-    copies = [pltpu.make_async_copy(dil_ref, next_dil_ref, sems.at[0])]
+    chip, core, _ = place()
+    small = [
+        pltpu.make_async_copy(dil_ref, next_dil_ref, sems.at[0]),
+        pltpu.make_async_copy(cols_ref, cols_buf, sems.at[33]),
+        pltpu.make_async_copy(phase_ref, phase_buf, sems.at[34]),
+    ]
+    copies = []
     for spin in range(4):
         for part in range(2):
             at = (spin, part)
@@ -124,8 +118,13 @@
                 at = (spin, part)
                 sem = sems.at[17 + which * 8 + spin * 2 + part]
                 next_copies.append(pltpu.make_async_copy(source.at[(core,) + at], target.at[at], sem))
-    for copy in copies + next_copies:
+    for copy in small + copies + next_copies:
         copy.start()
+    for copy in small:
+        copy.wait()
+    coef_ref[...] = coefficients(cols_buf[...], phase_buf[...])
+    dilution = jnp.broadcast_to(jnp.concatenate([next_dil_ref[...], next_dil_ref[...]], axis=1), (8, 128))
+    spin_ref[...] = lane_pick(dilution, lane_iota((8, 128)) ^ (chip & 15))
     for copy in copies:
         copy.wait()
     fill_rows(right_buf, next_dil_ref, rows_ref)
@@ -141,24 +140,33 @@
         add_tile(step, left_ref, rows_ref, out_ref)
 
 
-def products(left, right, dil):
+def products(left, right, dil, cols, phase):
     slot = (4, 2, 3, 128, 512)
     rows = pltpu.VMEM((320, 3072), jnp.bfloat16)
     whole = pltpu.VMEM((CHIPS * ROWS, 128), jnp.float32)
-    away, next_left, next_right, next_dil = pl.pallas_call(
+    away, next_left, next_right, next_dil, coef, spin_of = pl.pallas_call(
         away_kernel,
-        in_specs=[HBM_SPEC] * 3,
-        out_specs=[VMEM_SPEC] * 4,
-        out_shape=[whole, pltpu.VMEM(slot, jnp.bfloat16), pltpu.VMEM(slot, jnp.bfloat16), pltpu.VMEM((1, 64), jnp.int32)],
+        in_specs=[HBM_SPEC] * 5,
+        out_specs=[VMEM_SPEC] * 6,
+        out_shape=[
+            whole,
+            pltpu.VMEM(slot, jnp.bfloat16),
+            pltpu.VMEM(slot, jnp.bfloat16),
+            pltpu.VMEM((1, 64), jnp.int32),
+            pltpu.VMEM((32, 32), jnp.float32),
+            pltpu.VMEM((8, 128), jnp.int32),
+        ],
         scratch_shapes=[
             rows,
             pltpu.VMEM(slot, jnp.bfloat16),
             pltpu.VMEM(slot, jnp.bfloat16),
-            pltpu.SemaphoreType.DMA((33,)),
+            pltpu.VMEM((4, 16), jnp.int32),
+            pltpu.VMEM((4, 16), jnp.int32),
+            pltpu.SemaphoreType.DMA((35,)),
         ],
         compiler_params=pltpu.CompilerParams(vmem_limit_bytes=16 << 20),
         name="away",
-    )(*(pltpu.with_memory_space_constraint(x, pltpu.MemorySpace.HBM) for x in (left, right, dil)))
+    )(*(pltpu.with_memory_space_constraint(x, pltpu.MemorySpace.HBM) for x in (left, right, dil, cols, phase)))
     arrived = lax.ppermute(away, AXES, PARTNER)
     home = pl.pallas_call(
         home_kernel,
@@ -169,7 +177,7 @@
         compiler_params=pltpu.CompilerParams(vmem_limit_bytes=12 << 20),
         name="home",
     )(in_vmem(next_left), in_vmem(next_right), in_vmem(next_dil))
-    return call(add_kernel, "add", whole, in_vmem(home), in_vmem(arrived)), next_dil
+    return call(add_kernel, "add", whole, in_vmem(home), in_vmem(arrived)), coef, spin_of
 
 
 def add_kernel(a_ref, b_ref, out_ref):
@@ -182,41 +190,43 @@
         total = total + parts_ref[k * 160 : k * 160 + 160, :]
     for z in range(8):
         mine = total[z * ROWS : z * ROWS + ROWS]
-        out_ref[z * 40 : z * 40 + 40, :] = jnp.concatenate([mine, mine], axis=0)
+        out_ref[z * ROWS : z * ROWS + ROWS, :] = mine
+        out_ref[160 + z * ROWS : 160 + z * ROWS + ROWS, :] = mine
 
 
 def dot_exact(a, b, dims):
     return lax.dot_general(a, b, (dims, ((), ())), precision=EXACT, preferred_element_type=jnp.float32)
 
 
-def combine_kernel(parts_ref, cols_ref, phase_ref, dil_ref, pairs_ref, out_ref):
+def lane_pick(x, lanes):
+    return jnp.take_along_axis(x, lanes, axis=1)
+
+
+def combine_kernel(parts_ref, coef_ref, spin_ref, pairs_ref, out_ref):
     chip, core, _ = place()
-    coef = coefficients(cols_ref[...], phase_ref[...])
     lane8 = lane_iota((8, 128))
     row8 = row_iota((8, 128))
-    dilution = jnp.broadcast_to(jnp.concatenate([dil_ref[...], dil_ref[...]], axis=1), (8, 128))
-    spin_of = lane_xor(dilution, chip & 15, range(4))
-    noise_lane = lane8 >= 64
+    block = lane8 >> 4
+    turn = ((block + row8) & 7) * 16 + (lane8 & 15)
+    fall = (row8 - block) & 7
+    back = ((row8 - block) & 7) * 16 + (lane8 & 15)
+    spin_of = spin_ref[...]
     fields = []
-    total = parts_ref[0:40, :]
-    for z in range(1, 8):
-        total = total + parts_ref[z * 40 : z * 40 + 40, :]
     for time in range(2):
-        own = total[time * ROWS : time * ROWS + ROWS]
+        total = parts_ref[time * 160 : time * 160 + ROWS, :]
+        for z in range(1, 8):
+            at = time * 160 + z * ROWS
+            total = total + parts_ref[at : at + ROWS, :]
         terms = []
         for spin in range(4):
-            x = jnp.concatenate([own[spin * 4 : spin * 4 + 4], own[16:20]], axis=0)
-            for level in range(3):
-                row_bit = (row8 >> level) & 1
-                lane_bit = (lane8 >> (level + 4)) & 1
-                up = pltpu.roll(pltpu.roll(x, 1 << level, 0), 128 - (16 << level), 1)
-                down = pltpu.roll(pltpu.roll(x, 8 - (1 << level), 0), 16 << level, 1)
-                x = jnp.where(row_bit == lane_bit, x, jnp.where(row_bit == 1, up, down))
-            keep = jnp.logical_or(jnp.logical_not(noise_lane), spin_of == spin)
+            x = jnp.concatenate([total[spin * 4 : spin * 4 + 4], total[16:20]], axis=0)
+            x = lane_pick(jnp.take_along_axis(lane_pick(x, turn), fall, axis=0), back)
+            keep = jnp.logical_or(lane8 < 64, spin_of == spin)
             terms.append(jnp.where(keep, x, 0.0))
-        fields.append(dot_exact(coef, jnp.concatenate(terms, axis=0), ((0,), (0,))))
+        fields.append(dot_exact(coef_ref[...], jnp.concatenate(terms, axis=0), ((0,), (0,))))
     both = jnp.concatenate(fields, axis=0)
-    mirror = lane_xor(both, chip, range(7))
+    lanes = lane_iota((64, 128))
+    mirror = lane_pick(both, lanes ^ chip)
     cross = dot_exact(both, mirror, ((1,), (1,)))
     crossed = []
     for time in range(2):
@@ -234,8 +244,7 @@
             jnp.where(first, jnp.where(second, crossed[0], crossed[1]), jnp.where(second, crossed[2], crossed[3]))
         )
     trace_rows = jnp.concatenate(columns, axis=1)
-    ordered = lane_xor(both, chip & 112, range(4, 7))
-    ordered = jnp.where(core == 0, ordered, pltpu.roll(ordered, 120, 1))
+    ordered = lane_pick(both, ((lanes + 8 * core) & 127) ^ (chip & 112))
     lane = lane_iota((16, 128))
     for pair in range(8):
         rows = jnp.zeros((16, 128), jnp.float32)
@@ -259,9 +268,7 @@
         pieces.append(got_ref[pl.ds(at + 1, 8, stride=4), :])
     sums = jnp.sum(total, axis=0, keepdims=True)
     x = jnp.transpose(jnp.concatenate(pieces, axis=0))[0:32, :]
-    x = lane_xor(x, block * 8, range(3, 7))
-    for bit in range(3):
-        x = jnp.where(((row >> bit) & 1) != 0, lane_swap(x, 1 << bit), x)
+    x = lane_pick(x, lane_iota((32, 128)) ^ (block * 8 + (row & 7)))
     for time in range(2):
         for part in range(2):
             at = (time * 2 + part) * 8
@@ -307,7 +314,7 @@
     right = jnp.transpose(right_modes, (0, 1, 2, 4, 3, 5))
     dil = dilution.reshape(1, 64)
 
-    partial, dil = products(left, right, dil)
+    partial, coef, spin_of = products(left, right, dil, gamma_cols.T, gamma_phase.T)
     partial = partial.reshape(16, 160, 128)
     parts = lax.all_to_all(partial, AXES, 0, 0, axis_index_groups=PLANES, tiled=True)
     plane = call(sum_planes_kernel, "sum_planes", pltpu.VMEM((320, 128), jnp.float32), in_vmem(parts.reshape(2560, 128)))
@@ -317,9 +324,8 @@
         "combine",
         pltpu.VMEM((256, 128), jnp.float32),
         in_vmem(parts.reshape(320, 128)),
-        in_vmem(gamma_cols.T),
-        in_vmem(gamma_phase.T),
-        in_vmem(dil),
+        in_vmem(coef),
+        in_vmem(spin_of),
         in_vmem(time_pairs.T),
     )
     got = lax.all_to_all(rows.reshape(128, 2, 128), AXES, 0, 0, axis_index_groups=SAME_CORE, tiled=True)

time: 75.4 us -> 73.7 us (0.977)
  Pallas kernels: 10.5 us -> 9.48 us
    all_to_all x1, blocking collectives: 19.2 us -> 17.6 us  [local(): lax.all_to_all(plane.reshape(16, 1, 2560), AXES, 0, 0, axis_index_groups=...]
    all_to_all x1, blocking collectives: 16.8 us -> 17.9 us  [local(): lax.all_to_all(rows.reshape(128, 2, 128), AXES, 0, 0, axis_index_groups=S...]
where the time goes in v6:
time: 73.7 us; the launch traced here: 73.5 us
  blocking collectives  59.7 us (81%)
  Pallas kernels  9.48 us (13%)
  starting transfers between devices  3.29 us (4%)
    all_to_all x1, blocking collectives, local(): lax.all_to_all(partial, AXES, 0, 0, axis_index_groups=PLANES, tiled=True)  24.3 us
    all_to_all x1, blocking collectives, local(): lax.all_to_all(rows.reshape(128, 2, 128), AXES, 0, 0, axis_index_groups=S...  17.9 us
    all_to_all x1, blocking collectives, local(): lax.all_to_all(plane.reshape(16, 1, 2560), AXES, 0, 0, axis_index_groups=...  17.6 us
    pallas_call x1, Pallas kernels, products(): pl.pallas_call(away_kernel, in_specs=[HBM_SPEC] * 5, out_specs=[VMEM_SPEC...  5.41 us
    ppermute x1, starting transfers between devices, products(): arrived = lax.ppermute(away, AXES, PARTNER)  3.29 us
    pallas_call x1, Pallas kernels, products(): pl.pallas_call(home_kernel, in_specs=[VMEM_SPEC] * 3, out_specs=VMEM_SPEC...  2.3 us
  transfers between devices with their start and end apart: 1, of which 1 were waited for; matrix products, arithmetic and copies ran while one was open for 0% of the time, Pallas kernels for 3%

profile of v6, /device:TPU:1, one launch (start us, length us, event | category | flops | bytes accessed | tf_op | source)
XLA Modules:
  0.0 73.5 jit_solution(478920227693825974)
XLA Ops:
  0.6 5.4 %away.1 = (f32[2560,128]{1,0:T(8,128)S(1)}, bf16[4,2,3,128,512]{4,3,2,1,0:T(8,128)(2,1)S(1)}, bf16[4,2,3,128,512]{4,3,2,1,0:T(8,128)(2,1)S(1)}, s32[1,64]{1,0:T(...) custom-call(bf16[2,4,2,3,128,512]{5,4,3,2,1,0:T(8,128)(2,1)} %bitcast.20, ...), custom_call_target="tpu_custom_call" | custom-call | tf_op jit(solution)/shard_map/away/pallas_call | solution.py:147
  6.1 3.3 %collective-permute-start = (f32[2560,128]{1,0:T(8,128)S(1)}, f32[2560,128]{1,0:T(8,128)S(1)}, u32[]{:S(2)}, u32[]{:S(2)}) collective-permute-start(f32[2560,128]{1,0:T(8,128)S(1)} %get-tuple-element.13), channel_id=1, source_target_pairs={{0,16},{16,0},{2,18},{18,2},{4,20},{20,4},{6,22},{22,6},{8,24},{24... | collective-permute-start | bytes 3932168 | tf_op jit(solution)/shard_map/ppermute | solution.py:170
  9.3 2.3 %home.1.a_ref = f32[2560,128]{1,0:T(8,128)S(1)} custom-call(bf16[4,2,3,128,512]{4,3,2,1,0:T(8,128)(2,1)S(1)} %get-tuple-element.10.left_ref, bf16[4,2,3,128,512]{4,3,2,1,0:T(8,128)(2,1)S(1)} %get-tuple-element.11.right_ref, s32[1,64]{1,0:T(1,128)S(1)} %get-tuple-element.12.dil_ref), custom_call_target="tpu_custom_call" | custom-call | tf_op jit(solution)/shard_map/home/pallas_call | solution.py:171
  11.6 0.4 collective-permute-done.b_ref
  12.0 0.1 add.1
  12.1 24.3 %all_to_all.15 = f32[16,160,128]{2,1,0:T(8,128)S(1)} all-to-all(f32[16,160,128]{2,1,0:T(8,128)S(1)} %bitcast.14), channel_id=1, replica_groups={{0,32,64,96,1,33,65,97,128,160,192,224,129,161,193,225},{16,48,80,112,1..., dimensions={0} | all-to-all | bytes 2621440 | tf_op jit(solution)/shard_map/all_to_all | solution.py:319
  36.4 0.0 copy-start
  36.4 0.1 sum_planes.1
  36.5 17.6 %all_to_all.16 = f32[16,1,2560]{2,1,0:T(1,128)S(1)} all-to-all(f32[16,1,2560]{2,1,0:T(1,128)S(1)} %bitcast.16), channel_id=1, replica_groups={{0,2,4,6,8,10,12,14,16,18,20,22,24,26,28,30},{32,34,36,38,40,42,44,46,4..., dimensions={0} | all-to-all | bytes 327680 | tf_op jit(solution)/shard_map/all_to_all | solution.py:321
  54.0 0.0 copy-done
  54.0 0.8 %combine.1 = f32[256,128]{1,0:T(8,128)S(1)} custom-call(f32[320,128]{1,0:T(8,128)S(1)} %bitcast.15, f32[32,32]{1,0:T(8,128)S(1)} %get-tuple-element.14.coef_ref, s32[8,128]{1,0:T(8,128)S(1)} %get-tuple-element.15.spin_ref, s32[2,4]{1,0:T(2,128)S(1)} %bitcast.19), custom_call_target="tpu_custom_call" | custom-call | tf_op jit(solution)/shard_map/combine/pallas_call | solution.py:302
  54.9 17.9 %all_to_all.17 = f32[128,2,128]{2,1,0:T(2,128)S(1)} all-to-all(f32[128,2,128]{2,1,0:T(2,128)S(1)} %bitcast.17), channel_id=1, replica_groups={{0,1,2,3,4,5,6,7,8,9,10,11,12,13,14,15,32,33,34,35,36,37,38,39,40,41,42..., dimensions={0} | all-to-all | bytes 262144 | tf_op jit(solution)/shard_map/all_to_all | solution.py:331
  72.8 0.8 %finish.1 = (f32[1,2,2,8,128]{4,3,2,1,0:T(8,128)}, f32[4,1,2,16]{3,2,1,0:T(2,128)}) custom-call(f32[256,128]{1,0:T(8,128)S(1)} %bitcast.18), custom_call_target="tpu_custom_call" | custom-call | tf_op jit(solution)/shard_map/finish/pallas_call | solution.py:332
Async XLA Ops:
  6.1 6.0 %collective-permute-start = (f32[2560,128]{1,0:T(8,128)S(1)}, f32[2560,128]{1,0:T(8,128)S(1)}, u32[]{:S(2)}, u32[]{:S(2)}) collective-permute-start(f32[2560,128]{1,0:T(8,128)S(1)} %get-tuple-element.13), channel_id=1, source_target_pairs={{0,16},{16,0},{2,18},{18,2},{4,20},{20,4},{6,22},{22,6},{8,24},{24... | collective-permute-start | bytes 3932168 | tf_op jit(solution)/shard_map/ppermute | solution.py:170
  36.4 17.6 %copy-start = (s32[4,2]{0,1:T(2,128)S(1)}, s32[4,2]{0,1:T(2,128)}, u32[]{:S(2)}) copy-start(s32[4,2]{0,1:T(2,128)} %param.11) | copy-start | bytes 100

commit v7 on v6

--- a/solution.py
+++ b/solution.py
@@ -14,11 +14,11 @@
 
 def flat_index(chip, core):
     bit = [(chip >> k) & 1 for k in range(7)]
-    return bit[6] * 128 + bit[4] * 64 + bit[3] * 32 + core * 16 + (chip % 8) * 2 + bit[5]
-
-
-PLANES = [[flat_index(plane * 8 + z, core) for plane in range(16)] for z in range(8) for core in range(2)]
-COLUMNS = [[flat_index(plane * 8 + z, core) for core in range(2) for z in range(8)] for plane in range(16)]
+    return bit[6] * 128 + bit[4] * 64 + bit[3] * 32 + core * 16 + (chip & 3) * 4 + bit[2] * 2 + bit[5]
+
+
+BLOCKS = [[flat_index(block * 4 + z, core) for block in range(32)] for z in range(4) for core in range(2)]
+COLUMNS = [[flat_index(block * 4 + z, core) for core in range(2) for z in range(4)] for block in range(32)]
 PARTNER = [(flat_index(chip, core), flat_index(chip, 1 - core)) for chip in range(CHIPS) for core in range(2)]
 SAME_CORE = [sorted(flat_index(chip, core) for chip in range(CHIPS)) for core in range(2)]
 
@@ -33,24 +33,26 @@
 
 def place():
     gx, gy, gz = (lax.axis_index(name) for name in AXES)
-    chip = (gx >> 1) * 64 + (gz & 1) * 32 + (gx & 1) * 16 + (gy >> 1) * 8 + (gz >> 1)
+    chip = (gx >> 1) * 64 + (gz & 1) * 32 + (gx & 1) * 16 + (gy >> 1) * 8 + ((gz >> 1) & 1) * 4 + (gz >> 2)
     return chip, gy & 1, gx * 4 + gy
 
 
-def fill_rows(right_ref, dil_ref, rows_ref):
+def fill_pick(dil_ref, pick_ref):
     dilution = jnp.broadcast_to(jnp.concatenate([dil_ref[...], dil_ref[...]], axis=1), (128, 128))
     spin_of = jnp.transpose(dilution)[0:64, :]
-    pick = []
     for spin in range(4):
         one = jnp.where(spin_of == spin, 1.0, 0.0).astype(jnp.bfloat16)
-        pick.append(jnp.concatenate([one] * 4, axis=1))
+        pick_ref[spin] = jnp.concatenate([one] * 4, axis=1)
+
+
+def fill_rows(right_ref, pick_ref, rows_ref):
     for part in range(2):
         for colour in range(3):
             at = (part * 3 + colour) * 512
             noise = None
             for spin in range(4):
                 rows_ref[spin * 64 : spin * 64 + 64, at : at + 512] = right_ref[spin, part, colour, 0:64, :]
-                term = right_ref[spin, part, colour, 64:128, :] * pick[spin]
+                term = right_ref[spin, part, colour, 64:128, :] * pick_ref[spin]
                 noise = term if noise is None else noise + term
             rows_ref[256:320, at : at + 512] = noise
 
@@ -91,12 +93,12 @@
 
 
 def away_kernel(
-    left_ref, right_ref, dil_ref, cols_ref, phase_ref, out_ref, next_left_ref, next_right_ref, next_dil_ref, coef_ref, spin_ref,
-    rows_ref, left_buf, right_buf, cols_buf, phase_buf, sems
+    left_ref, right_ref, dil_ref, cols_ref, phase_ref, out_ref, next_left_ref, next_right_ref, pick_ref, coef_ref, spin_ref,
+    rows_ref, left_buf, right_buf, dil_buf, cols_buf, phase_buf, sems
 ):
     chip, core, _ = place()
     small = [
-        pltpu.make_async_copy(dil_ref, next_dil_ref, sems.at[0]),
+        pltpu.make_async_copy(dil_ref, dil_buf, sems.at[0]),
         pltpu.make_async_copy(cols_ref, cols_buf, sems.at[33]),
         pltpu.make_async_copy(phase_ref, phase_buf, sems.at[34]),
     ]
@@ -122,20 +124,21 @@
         copy.start()
     for copy in small:
         copy.wait()
+    fill_pick(dil_buf, pick_ref)
     coef_ref[...] = coefficients(cols_buf[...], phase_buf[...])
-    dilution = jnp.broadcast_to(jnp.concatenate([next_dil_ref[...], next_dil_ref[...]], axis=1), (8, 128))
+    dilution = jnp.broadcast_to(jnp.concatenate([dil_buf[...], dil_buf[...]], axis=1), (8, 128))
     spin_ref[...] = lane_pick(dilution, lane_iota((8, 128)) ^ (chip & 15))
     for copy in copies:
         copy.wait()
-    fill_rows(right_buf, next_dil_ref, rows_ref)
+    fill_rows(right_buf, pick_ref, rows_ref)
     for step in range(4):
         add_tile(step, left_buf, rows_ref, out_ref)
     for copy in next_copies:
         copy.wait()
 
 
-def home_kernel(left_ref, right_ref, dil_ref, out_ref, rows_ref):
-    fill_rows(right_ref, dil_ref, rows_ref)
+def home_kernel(left_ref, right_ref, pick_ref, out_ref, rows_ref):
+    fill_rows(right_ref, pick_ref, rows_ref)
     for step in range(4):
         add_tile(step, left_ref, rows_ref, out_ref)
 
@@ -144,7 +147,7 @@
     slot = (4, 2, 3, 128, 512)
     rows = pltpu.VMEM((320, 3072), jnp.bfloat16)
     whole = pltpu.VMEM((CHIPS * ROWS, 128), jnp.float32)
-    away, next_left, next_right, next_dil, coef, spin_of = pl.pallas_call(
+    away, next_left, next_right, pick, coef, spin_of = pl.pallas_call(
         away_kernel,
         in_specs=[HBM_SPEC] * 5,
         out_specs=[VMEM_SPEC] * 6,
@@ -152,7 +155,7 @@
             whole,
             pltpu.VMEM(slot, jnp.bfloat16),
             pltpu.VMEM(slot, jnp.bfloat16),
-            pltpu.VMEM((1, 64), jnp.int32),
+            pltpu.VMEM((4, 64, 512), jnp.bfloat16),
             pltpu.VMEM((32, 32), jnp.float32),
             pltpu.VMEM((8, 128), jnp.int32),
         ],
@@ -160,6 +163,7 @@
             rows,
             pltpu.VMEM(slot, jnp.bfloat16),
             pltpu.VMEM(slot, jnp.bfloat16),
+            pltpu.VMEM((1, 64), jnp.int32),
             pltpu.VMEM((4, 16), jnp.int32),
             pltpu.VMEM((4, 16), jnp.int32),
             pltpu.SemaphoreType.DMA((35,)),
@@ -176,7 +180,7 @@
         scratch_shapes=[rows],
         compiler_params=pltpu.CompilerParams(vmem_limit_bytes=12 << 20),
         name="home",
-    )(in_vmem(next_left), in_vmem(next_right), in_vmem(next_dil))
+    )(in_vmem(next_left), in_vmem(next_right), in_vmem(pick))
     return call(add_kernel, "add", whole, in_vmem(home), in_vmem(arrived)), coef, spin_of
 
 
@@ -184,14 +188,12 @@
     out_ref[...] = a_ref[...] + b_ref[...]
 
 
-def sum_planes_kernel(parts_ref, out_ref):
-    total = parts_ref[0:160, :]
-    for k in range(1, 16):
-        total = total + parts_ref[k * 160 : k * 160 + 160, :]
-    for z in range(8):
-        mine = total[z * ROWS : z * ROWS + ROWS]
-        out_ref[z * ROWS : z * ROWS + ROWS, :] = mine
-        out_ref[160 + z * ROWS : 160 + z * ROWS + ROWS, :] = mine
+def sum_blocks_kernel(parts_ref, out_ref):
+    total = parts_ref[0:80, :]
+    for k in range(1, 32):
+        total = total + parts_ref[k * 80 : k * 80 + 80, :]
+    out_ref[0:80, :] = total
+    out_ref[80:160, :] = total
 
 
 def dot_exact(a, b, dims):
@@ -213,9 +215,9 @@
     spin_of = spin_ref[...]
     fields = []
     for time in range(2):
-        total = parts_ref[time * 160 : time * 160 + ROWS, :]
-        for z in range(1, 8):
-            at = time * 160 + z * ROWS
+        total = parts_ref[time * 80 : time * 80 + ROWS, :]
+        for z in range(1, 4):
+            at = time * 80 + z * ROWS
             total = total + parts_ref[at : at + ROWS, :]
         terms = []
         for spin in range(4):
@@ -263,9 +265,10 @@
     for high in range(16):
         x_high, y_high, x_low, y_low = ((high >> k) & 1 for k in (3, 2, 1, 0))
         at = (x_high * 4 + x_low * 2 + y_low) * 32 + y_high * 2
-        piece = got_ref[pl.ds(at, 8, stride=4), :]
-        total = piece if total is None else total + piece
-        pieces.append(got_ref[pl.ds(at + 1, 8, stride=4), :])
+        for odd in range(2):
+            piece = got_ref[pl.ds(at + odd * 4, 4, stride=8), :]
+            total = piece if total is None else total + piece
+            pieces.append(got_ref[pl.ds(at + odd * 4 + 1, 4, stride=8), :])
     sums = jnp.sum(total, axis=0, keepdims=True)
     x = jnp.transpose(jnp.concatenate(pieces, axis=0))[0:32, :]
     x = lane_pick(x, lane_iota((32, 128)) ^ (block * 8 + (row & 7)))
@@ -315,15 +318,15 @@
     dil = dilution.reshape(1, 64)
 
     partial, coef, spin_of = products(left, right, dil, gamma_cols.T, gamma_phase.T)
-    partial = partial.reshape(16, 160, 128)
-    parts = lax.all_to_all(partial, AXES, 0, 0, axis_index_groups=PLANES, tiled=True)
-    plane = call(sum_planes_kernel, "sum_planes", pltpu.VMEM((320, 128), jnp.float32), in_vmem(parts.reshape(2560, 128)))
-    parts = lax.all_to_all(plane.reshape(16, 1, 2560), AXES, 0, 0, axis_index_groups=COLUMNS, tiled=True)
+    partial = partial.reshape(32, 80, 128)
+    parts = lax.all_to_all(partial, AXES, 0, 0, axis_index_groups=BLOCKS, tiled=True)
+    plane = call(sum_blocks_kernel, "sum_blocks", pltpu.VMEM((160, 128), jnp.float32), in_vmem(parts.reshape(2560, 128)))
+    parts = lax.all_to_all(plane.reshape(8, 1, 2560), AXES, 0, 0, axis_index_groups=COLUMNS, tiled=True)
     rows = call(
         combine_kernel,
         "combine",
         pltpu.VMEM((256, 128), jnp.float32),
-        in_vmem(parts.reshape(320, 128)),
+        in_vmem(parts.reshape(160, 128)),
         in_vmem(coef),
         in_vmem(spin_of),
         in_vmem(time_pairs.T),

time: 73.7 us -> 73.7 us (level)
    all_to_all x2, blocking collectives: 41.8 us -> 43.2 us  [the longest x1 26.3 us: local(): lax.all_to_all(partial, AXES, 0, 0, axis_index_groups=BLOCKS, tiled=True)]
    all_to_all x1, blocking collectives: 17.9 us -> 16.6 us  [local(): lax.all_to_all(rows.reshape(128, 2, 128), AXES, 0, 0, axis_index_groups=S...]
where the time goes in v7:
time: 73.7 us; the launch traced here: 73.5 us
  blocking collectives  59.8 us (81%)
  Pallas kernels  9.48 us (13%)
  starting transfers between devices  3.29 us (4%)
    all_to_all x1, blocking collectives, local(): lax.all_to_all(partial, AXES, 0, 0, axis_index_groups=BLOCKS, tiled=True)  26.3 us
    all_to_all x1, blocking collectives, local(): lax.all_to_all(plane.reshape(8, 1, 2560), AXES, 0, 0, axis_index_groups=C...  16.9 us
    all_to_all x1, blocking collectives, local(): lax.all_to_all(rows.reshape(128, 2, 128), AXES, 0, 0, axis_index_groups=S...  16.6 us
    pallas_call x1, Pallas kernels, products(): pl.pallas_call(away_kernel, in_specs=[HBM_SPEC] * 5, out_specs=[VMEM_SPEC...  5.38 us
    ppermute x1, starting transfers between devices, products(): arrived = lax.ppermute(away, AXES, PARTNER)  3.29 us
    pallas_call x1, Pallas kernels, products(): pl.pallas_call(home_kernel, in_specs=[VMEM_SPEC] * 3, out_specs=VMEM_SPEC...  2.31 us
  transfers between devices with their start and end apart: 1, of which 1 were waited for; matrix products, arithmetic and copies ran while one was open for 0% of the time, Pallas kernels for 3%

profile of v7, /device:TPU:1, one launch (start us, length us, event | category | flops | bytes accessed | tf_op | source)
XLA Modules:
  0.0 73.5 jit_solution(13273646199228085258)
XLA Ops:
  0.6 5.4 %away.1 = (f32[2560,128]{1,0:T(8,128)S(1)}, bf16[4,2,3,128,512]{4,3,2,1,0:T(8,128)(2,1)S(1)}, bf16[4,2,3,128,512]{4,3,2,1,0:T(8,128)(2,1)S(1)}, bf16[4,64,512]{2...) custom-call(bf16[2,4,2,3,128,512]{5,4,3,2,1,0:T(8,128)(2,1)} %bitcast.20, ...), custom_call_target="tpu_custom_call" | custom-call | tf_op jit(solution)/shard_map/away/pallas_call | solution.py:150
  6.0 3.3 %collective-permute-start = (f32[2560,128]{1,0:T(8,128)S(1)}, f32[2560,128]{1,0:T(8,128)S(1)}, u32[]{:S(2)}, u32[]{:S(2)}) collective-permute-start(f32[2560,128]{1,0:T(8,128)S(1)} %get-tuple-element.13), channel_id=1, source_target_pairs={{0,16},{16,0},{4,20},{20,4},{8,24},{24,8},{12,28},{28,12},{2,18},{... | collective-permute-start | bytes 3932168 | tf_op jit(solution)/shard_map/ppermute | solution.py:174
  9.3 2.3 %home.1.a_ref = f32[2560,128]{1,0:T(8,128)S(1)} custom-call(bf16[4,2,3,128,512]{4,3,2,1,0:T(8,128)(2,1)S(1)} %get-tuple-element.10.left_ref, bf16[4,2,3,128,512]{4,3,2,1,0:T(8,128)(2,1)S(1)} %get-tuple-element.11.right_ref, bf16[4,64,512]{2,1,0:T(8,128)(2,1)S(1)} %get-tuple-element.12.pick_ref), custom_call_target="tpu_custom_call" | custom-call | tf_op jit(solution)/shard_map/home/pallas_call | solution.py:175
  11.6 0.3 collective-permute-done.b_ref
  12.0 0.1 add.1
  12.1 26.3 %all_to_all.15 = f32[32,80,128]{2,1,0:T(8,128)S(1)} all-to-all(f32[32,80,128]{2,1,0:T(8,128)S(1)} %bitcast.14), channel_id=1, replica_groups={{0,2,32,34,64,66,96,98,1,3,33,35,65,67,97,99,128,130,160,162,192,194,22..., dimensions={0} | all-to-all | bytes 2621440 | tf_op jit(solution)/shard_map/all_to_all | solution.py:322
  38.4 0.0 copy-start
  38.4 0.1 sum_blocks.1
  38.5 16.9 %all_to_all.16 = f32[8,1,2560]{2,1,0:T(1,128)S(1)} all-to-all(f32[8,1,2560]{2,1,0:T(1,128)S(1)} %bitcast.18), channel_id=1, replica_groups={{0,4,8,12,16,20,24,28},{2,6,10,14,18,22,26,30},{32,36,40,44,48,52,56,60..., dimensions={0} | all-to-all | bytes 163840 | tf_op jit(solution)/shard_map/all_to_all | solution.py:324
  55.4 0.0 copy-done
  55.4 0.8 %combine.1 = f32[256,128]{1,0:T(8,128)S(1)} custom-call(f32[160,128]{1,0:T(8,128)S(1)} %bitcast.17, f32[32,32]{1,0:T(8,128)S(1)} %get-tuple-element.14.coef_ref, s32[8,128]{1,0:T(8,128)S(1)} %get-tuple-element.15.spin_ref, s32[2,4]{1,0:T(2,128)S(1)} %bitcast.19), custom_call_target="tpu_custom_call" | custom-call | tf_op jit(solution)/shard_map/combine/pallas_call | solution.py:305
  56.2 16.6 %all_to_all.17 = f32[128,2,128]{2,1,0:T(2,128)S(1)} all-to-all(f32[128,2,128]{2,1,0:T(2,128)S(1)} %bitcast.15), channel_id=1, replica_groups={{0,1,2,3,4,5,6,7,8,9,10,11,12,13,14,15,32,33,34,35,36,37,38,39,40,41,42..., dimensions={0} | all-to-all | bytes 262144 | tf_op jit(solution)/shard_map/all_to_all | solution.py:334
  72.8 0.8 %finish.1 = (f32[1,2,2,8,128]{4,3,2,1,0:T(8,128)}, f32[4,1,2,16]{3,2,1,0:T(2,128)}) custom-call(f32[256,128]{1,0:T(8,128)S(1)} %bitcast.16), custom_call_target="tpu_custom_call" | custom-call | tf_op jit(solution)/shard_map/finish/pallas_call | solution.py:335
Async XLA Ops:
  6.0 5.9 %collective-permute-start = (f32[2560,128]{1,0:T(8,128)S(1)}, f32[2560,128]{1,0:T(8,128)S(1)}, u32[]{:S(2)}, u32[]{:S(2)}) collective-permute-start(f32[2560,128]{1,0:T(8,128)S(1)} %get-tuple-element.13), channel_id=1, source_target_pairs={{0,16},{16,0},{4,20},{20,4},{8,24},{24,8},{12,28},{28,12},{2,18},{... | collective-permute-start | bytes 3932168 | tf_op jit(solution)/shard_map/ppermute | solution.py:174
  38.4 17.0 %copy-start = (s32[4,2]{0,1:T(2,128)S(1)}, s32[4,2]{0,1:T(2,128)}, u32[]{:S(2)}) copy-start(s32[4,2]{0,1:T(2,128)} %param.11) | copy-start | bytes 100

commit v8 on v7

--- a/solution.py
+++ b/solution.py
@@ -6,7 +6,6 @@
 from jax.sharding import PartitionSpec as P
 
 AXES = ("gx", "gy", "gz")
-EXACT = lax.Precision.HIGHEST
 CHIPS = 128
 ROWS = 20
 VMEM = pltpu.MemorySpace.VMEM
@@ -196,8 +195,15 @@
     out_ref[80:160, :] = total
 
 
-def dot_exact(a, b, dims):
-    return lax.dot_general(a, b, (dims, ((), ())), precision=EXACT, preferred_element_type=jnp.float32)
+def split(x):
+    high = x.astype(jnp.bfloat16)
+    rest = x - high.astype(jnp.float32)
+    middle = rest.astype(jnp.bfloat16)
+    return high, middle, (rest - middle.astype(jnp.float32)).astype(jnp.bfloat16)
+
+
+def dot(a, b, dims):
+    return lax.dot_general(a, b, (dims, ((), ())), preferred_element_type=jnp.float32)
 
 
 def lane_pick(x, lanes):
@@ -213,6 +219,7 @@
     fall = (row8 - block) & 7
     back = ((row8 - block) & 7) * 16 + (lane8 & 15)
     spin_of = spin_ref[...]
+    coef = jnp.concatenate([coef_ref[...].astype(jnp.bfloat16)] * 3, axis=0)
     fields = []
     for time in range(2):
         total = parts_ref[time * 80 : time * 80 + ROWS, :]
@@ -225,11 +232,18 @@
             x = lane_pick(jnp.take_along_axis(lane_pick(x, turn), fall, axis=0), back)
             keep = jnp.logical_or(lane8 < 64, spin_of == spin)
             terms.append(jnp.where(keep, x, 0.0))
-        fields.append(dot_exact(coef_ref[...], jnp.concatenate(terms, axis=0), ((0,), (0,))))
+        parts = jnp.concatenate(split(jnp.concatenate(terms, axis=0)), axis=0)
+        fields.append(dot(coef, parts, ((0,), (0,))))
     both = jnp.concatenate(fields, axis=0)
     lanes = lane_iota((64, 128))
     mirror = lane_pick(both, lanes ^ chip)
-    cross = dot_exact(both, mirror, ((1,), (1,)))
+    a_high, a_middle, a_low = split(both)
+    b_high, b_middle, b_low = split(mirror)
+    cross = dot(
+        jnp.concatenate([a_low, a_high, a_middle, a_middle, a_high, a_high], axis=1),
+        jnp.concatenate([b_high, b_low, b_middle, b_high, b_middle, b_high], axis=1),
+        ((1,), (1,)),
+    )
     crossed = []
     for time in range(2):
         real = cross[time * 32 : time * 32 + 16]

time: 73.7 us -> 73.6 us (level)
  no operation moved by 1% of the time
where the time goes in v8:
time: 73.6 us; the launch traced here: 73.4 us
  blocking collectives  59.8 us (81%)
  Pallas kernels  9.39 us (13%)
  starting transfers between devices  3.29 us (4%)
    all_to_all x1, blocking collectives, local(): lax.all_to_all(partial, AXES, 0, 0, axis_index_groups=BLOCKS, tiled=True)  26.3 us
    all_to_all x1, blocking collectives, local(): lax.all_to_all(plane.reshape(8, 1, 2560), AXES, 0, 0, axis_index_groups=C...  16.9 us
    all_to_all x1, blocking collectives, local(): lax.all_to_all(rows.reshape(128, 2, 128), AXES, 0, 0, axis_index_groups=S...  16.6 us
    pallas_call x1, Pallas kernels, products(): pl.pallas_call(away_kernel, in_specs=[HBM_SPEC] * 5, out_specs=[VMEM_SPEC...  5.38 us
    ppermute x1, starting transfers between devices, products(): arrived = lax.ppermute(away, AXES, PARTNER)  3.29 us
    pallas_call x1, Pallas kernels, products(): pl.pallas_call(home_kernel, in_specs=[VMEM_SPEC] * 3, out_specs=VMEM_SPEC...  2.31 us
  transfers between devices with their start and end apart: 1, of which 1 were waited for; matrix products, arithmetic and copies ran while one was open for 0% of the time, Pallas kernels for 3%

profile of v8, /device:TPU:1, one launch (start us, length us, event | category | flops | bytes accessed | tf_op | source)
XLA Modules:
  0.0 73.4 jit_solution(1032260455562659442)
XLA Ops:
  0.6 5.4 %away.1 = (f32[2560,128]{1,0:T(8,128)S(1)}, bf16[4,2,3,128,512]{4,3,2,1,0:T(8,128)(2,1)S(1)}, bf16[4,2,3,128,512]{4,3,2,1,0:T(8,128)(2,1)S(1)}, bf16[4,64,512]{2...) custom-call(bf16[2,4,2,3,128,512]{5,4,3,2,1,0:T(8,128)(2,1)} %bitcast.20, ...), custom_call_target="tpu_custom_call" | custom-call | tf_op jit(solution)/shard_map/away/pallas_call | solution.py:149
  6.0 3.3 %collective-permute-start = (f32[2560,128]{1,0:T(8,128)S(1)}, f32[2560,128]{1,0:T(8,128)S(1)}, u32[]{:S(2)}, u32[]{:S(2)}) collective-permute-start(f32[2560,128]{1,0:T(8,128)S(1)} %get-tuple-element.13), channel_id=1, source_target_pairs={{0,16},{16,0},{4,20},{20,4},{8,24},{24,8},{12,28},{28,12},{2,18},{... | collective-permute-start | bytes 3932168 | tf_op jit(solution)/shard_map/ppermute | solution.py:173
  9.3 2.3 %home.1.a_ref = f32[2560,128]{1,0:T(8,128)S(1)} custom-call(bf16[4,2,3,128,512]{4,3,2,1,0:T(8,128)(2,1)S(1)} %get-tuple-element.10.left_ref, bf16[4,2,3,128,512]{4,3,2,1,0:T(8,128)(2,1)S(1)} %get-tuple-element.11.right_ref, bf16[4,64,512]{2,1,0:T(8,128)(2,1)S(1)} %get-tuple-element.12.pick_ref), custom_call_target="tpu_custom_call" | custom-call | tf_op jit(solution)/shard_map/home/pallas_call | solution.py:174
  11.6 0.3 collective-permute-done.b_ref
  12.0 0.1 add.1
  12.1 26.3 %all_to_all.15 = f32[32,80,128]{2,1,0:T(8,128)S(1)} all-to-all(f32[32,80,128]{2,1,0:T(8,128)S(1)} %bitcast.14), channel_id=1, replica_groups={{0,2,32,34,64,66,96,98,1,3,33,35,65,67,97,99,128,130,160,162,192,194,22..., dimensions={0} | all-to-all | bytes 2621440 | tf_op jit(solution)/shard_map/all_to_all | solution.py:336
  38.4 0.0 copy-start
  38.4 0.1 sum_blocks.1
  38.5 16.9 %all_to_all.16 = f32[8,1,2560]{2,1,0:T(1,128)S(1)} all-to-all(f32[8,1,2560]{2,1,0:T(1,128)S(1)} %bitcast.18), channel_id=1, replica_groups={{0,4,8,12,16,20,24,28},{2,6,10,14,18,22,26,30},{32,36,40,44,48,52,56,60..., dimensions={0} | all-to-all | bytes 163840 | tf_op jit(solution)/shard_map/all_to_all | solution.py:338
  55.4 0.0 copy-done
  55.4 0.7 combine.1
  56.1 16.6 %all_to_all.17 = f32[128,2,128]{2,1,0:T(2,128)S(1)} all-to-all(f32[128,2,128]{2,1,0:T(2,128)S(1)} %bitcast.15), channel_id=1, replica_groups={{0,1,2,3,4,5,6,7,8,9,10,11,12,13,14,15,32,33,34,35,36,37,38,39,40,41,42..., dimensions={0} | all-to-all | bytes 262144 | tf_op jit(solution)/shard_map/all_to_all | solution.py:348
  72.7 0.8 %finish.1 = (f32[1,2,2,8,128]{4,3,2,1,0:T(8,128)}, f32[4,1,2,16]{3,2,1,0:T(2,128)}) custom-call(f32[256,128]{1,0:T(8,128)S(1)} %bitcast.16), custom_call_target="tpu_custom_call" | custom-call | tf_op jit(solution)/shard_map/finish/pallas_call | solution.py:349
Async XLA Ops:
  6.0 5.9 %collective-permute-start = (f32[2560,128]{1,0:T(8,128)S(1)}, f32[2560,128]{1,0:T(8,128)S(1)}, u32[]{:S(2)}, u32[]{:S(2)}) collective-permute-start(f32[2560,128]{1,0:T(8,128)S(1)} %get-tuple-element.13), channel_id=1, source_target_pairs={{0,16},{16,0},{4,20},{20,4},{8,24},{24,8},{12,28},{28,12},{2,18},{... | collective-permute-start | bytes 3932168 | tf_op jit(solution)/shard_map/ppermute | solution.py:173
  38.4 17.0 %copy-start = (s32[4,2]{0,1:T(2,128)S(1)}, s32[4,2]{0,1:T(2,128)}, u32[]{:S(2)}) copy-start(s32[4,2]{0,1:T(2,128)} %param.11) | copy-start | bytes 100
